TPU v7x, 16 devices: a 4x2x1 block of a 4x4x8 slice. The times are simulated.
16 devices in a mesh: rep: 4 (over y, z, core), dp: 4 (over x).
Axes of the slice: x: 4, y: 2, z: 1, core: 2. Of those that a mesh axis runs over, the one named last changes fastest.
The devices are a block of a 4x4x8 slice.
Arguments:
- x: bfloat16 [16, 4096, 1024], P(('rep', 'dp')), parts along dimension 0
- dy: bfloat16 [16, 4096, 1024], P(('rep', 'dp')), parts along dimension 0
- w_gate: bfloat16 [2, 1024, 3200], P(None, 'dp')
- w_up: bfloat16 [2, 1024, 3200], P(None, 'dp')
- w_down: bfloat16 [2, 3200, 1024], P(None, 'dp')
- m_w_gate: float32 [2, 1024, 3200], P(None, 'dp')
- m_w_up: float32 [2, 1024, 3200], P(None, 'dp')
- m_w_down: float32 [2, 3200, 1024], P(None, 'dp')
- v_w_gate: float32 [2, 1024, 3200], P(None, 'dp')
- v_w_up: float32 [2, 1024, 3200], P(None, 'dp')
- v_w_down: float32 [2, 3200, 1024], P(None, 'dp')
Outputs:
- output 1: bfloat16 [8, 1024, 3200], P('rep', 'dp'), parts along dimension 0
- output 2: bfloat16 [8, 1024, 3200], P('rep', 'dp'), parts along dimension 0
- output 3: bfloat16 [8, 3200, 1024], P('rep', 'dp'), parts along dimension 0
- output 4: float32 [8, 1024, 3200], P('rep', 'dp'), parts along dimension 0
- output 5: float32 [8, 1024, 3200], P('rep', 'dp'), parts along dimension 0
- output 6: float32 [8, 3200, 1024], P('rep', 'dp'), parts along dimension 0
- output 7: float32 [8, 1024, 3200], P('rep', 'dp'), parts along dimension 0
- output 8: float32 [8, 1024, 3200], P('rep', 'dp'), parts along dimension 0
- output 9: float32 [8, 3200, 1024], P('rep', 'dp'), parts along dimension 0
There are 4 independent parts. A program takes and returns all parts, laid end to end along the dimension named above; an argument that names none is the same for every part.
All inputs are finite; a program needn't handle non-finite values.
Results may differ from a plain program's by a relative error of at most 0.022.
Values are sent between devices in bfloat16 or wider.
A program may use at most 768 MiB of HBM per device.

v0:
```python
import jax
import jax.numpy as jnp
from jax import lax
from jax.sharding import PartitionSpec as P

NAMES = ("w_gate", "w_up", "w_down")


def matmul(a, w):
    return jnp.dot(a, w, preferred_element_type=jnp.float32).astype(jnp.bfloat16)


def normed(h):
    wide = h.astype(jnp.float32)
    scale = lax.rsqrt(jnp.mean(wide**2, -1, keepdims=True) + 1e-6)
    return (wide * scale).astype(jnp.bfloat16)


def layer(h, w):
    a = normed(h)
    gate = jnp.dot(a, w["w_gate"], preferred_element_type=jnp.float32)
    up = jnp.dot(a, w["w_up"], preferred_element_type=jnp.float32)
    return h + matmul((jax.nn.silu(gate) * up).astype(jnp.bfloat16), w["w_down"])


def adamw(w, m, v, g):
    m = 0.9 * m + 0.1 * g
    v = 0.95 * v + 0.05 * g * g
    step = m * lax.rsqrt(v + 1e-8) + 0.1 * w
    return (w - 0.02 * step).astype(jnp.bfloat16), m, v


def clipped(gradients, sum_of_squares, count):
    factor = jnp.minimum(1.0, 0.5 * lax.rsqrt(sum_of_squares / count + 1e-30))
    return [g * factor for g in gradients]


def solution(mesh):
    def fetched(weights, number):
        return {name: lax.all_gather(w[number], "dp", axis=0, tiled=True) for name, w in zip(NAMES, weights, strict=True)}

    def step(x, dy, *arrays):
        weights, m, v = (arrays[i : i + 3] for i in (0, 3, 6))
        layers = weights[0].shape[0]
        h, kept = x[0], []
        for number in range(layers):
            kept.append(h)
            h = layer(h, fetched(weights, number))
        by_h, mine = dy[0], [None] * layers
        for number in reversed(range(layers)):
            _, back = jax.vjp(lambda w, h: layer(h, w), fetched(weights, number), kept[number])
            by_w, by_h = back(by_h)
            mine[number] = [lax.psum_scatter(by_w[name], "dp", scatter_dimension=0, tiled=True) for name in NAMES]
        gradients = [jnp.stack([mine[number][i] for number in range(layers)]).astype(jnp.float32) for i in range(3)]
        squares = lax.psum(sum(jnp.sum(g * g) for g in gradients), "dp")
        gradients = clipped(gradients, squares, lax.psum(1, "dp") * sum(g.size for g in gradients))
        new = [adamw(w.astype(jnp.float32), m, v, g) for w, m, v, g in zip(weights, m, v, gradients, strict=True)]
        return tuple(one[which] for which in range(3) for one in new)

    states, cut = P(("rep", "dp"), None, None), P(None, "dp", None)
    return jax.shard_map(
        step,
        mesh=mesh,
        in_specs=(states, states) + (cut,) * 9,
        out_specs=(P("rep", "dp", None),) * 9,
        check_vma=False,
    )
```

profile of v0, /device:TPU:112, one launch (start us, length us, event | category | flops | bytes accessed | tf_op | source)
XLA Modules:
  0.0 1047.0 jit_solution(798338399297762541)
XLA Ops:
  48.2 29.9 %all-gather.13.cloned.1.call-done = bf16[1,1024,3200]{2,1,0:T(8,128)(2,1)} async-done(((bf16[1,256,3200]{2,1,0:T(8,128)(2,1)}), bf16[1,1024,3200]{2,1,0:T(8,128)(2,1)}) %all-gather.13.cloned.1.call-update) | async-done | bytes 6553616 | tf_op jit(solution)/shard_map/all_gather | solution.py:40
  78.2 37.6 %fusion.67 = f32[4096,3200]{1,0:T(8,128)} fusion(bf16[1,1024,3200]{2,1,0:T(8,128)(2,1)} %all-gather.13.cloned.1.call-done, bf16[1,4096,1024]{1,2,0:T(8,128)(2,1)} %copy.20, f32[4096]{0:T(1024)S(1)} %add_rsqrt_fusion), kind=kOutput, calls=%fused_computation.99 | convolution fusion | flops 26856128512 | bytes 67387392 | tf_op jit(solution)/shard_map/dot_general | solution.py:21
  115.8 29.1 %all-gather.15.cloned.1.call-done = bf16[1,1024,3200]{2,1,0:T(8,128)(2,1)} async-done(((bf16[1,256,3200]{2,1,0:T(8,128)(2,1)}), bf16[1,1024,3200]{2,1,0:T(8,128)(2,1)}) %all-gather.15.cloned.1.call-update) | async-done | bytes 6553616 | tf_op jit(solution)/shard_map/all_gather | solution.py:40
  144.8 58.1 %multiply_convert_fusion.1 = (bf16[4096,3200]{1,0:T(8,128)(2,1)}, f32[4096,3200]{1,0:T(8,128)}) fusion(f32[4096,3200]{1,0:T(8,128)} %fusion.67, bf16[1,1024,3200]{2,1,0:T(8,128)(2,1)} %all-gather.15.cloned.1.call-done, bf16[1,4096,1024]{1,2,0:T(8,128)(2,1)} %copy.20, f32[4096]{0:T(1024)S(1)} %add_rsqrt_fusion), kind=kOutput, calls=%fused_computation.17 | convolution fusion | flops 26934771712 | bytes 146030592 | tf_op jit(solution)/shard_map/dot_general | solution.py:22
  211.5 37.3 %fusion.19 = (f32[4096]{0:T(1024)S(1)}, bf16[4096,1024]{0,1:T(8,128)(2,1)}) fusion(bf16[4096,3200]{1,0:T(8,128)(2,1)} %get-tuple-element.24, bf16[1,3200,1024]{2,1,0:T(8,128)(2,1)} %all-gather.17.cloned.1.call-done, bf16[1,4096,1024]{1,2,0:T(8,128)(2,1)} %copy.20), kind=kOutput, calls=%fused_computation.37 | convolution fusion | flops 26864513024 | bytes 49561600 | tf_op jit(solution)/shard_map/dot_general | solution.py:10
  248.8 29.2 %all-gather.21.cloned.1.call-done = bf16[1,3200,1024]{2,1,0:T(8,128)(2,1)} async-done(((bf16[1,800,1024]{2,1,0:T(8,128)(2,1)}), bf16[1,3200,1024]{2,1,0:T(8,128)(2,1)}) %all-gather.21.cloned.1.call-update) | async-done | bytes 6553616 | tf_op jit(solution)/shard_map/all_gather | solution.py:40
  278.0 36.4 %convolution_convert_fusion.1 = bf16[4096,3200]{1,0:T(8,128)(2,1)} fusion(bf16[1,4096,1024]{2,1,0:T(8,128)(2,1)} %param.12, bf16[1,3200,1024]{2,1,0:T(8,128)(2,1)} %all-gather.21.cloned.1.call-done), kind=kOutput, calls=%fused_computation.23 | convolution fusion | flops 26856652800 | bytes 41156608 | tf_op jit(solution)/shard_map/transpose(jvp())/dot_general | solution.py:10
  314.4 30.1 %all-gather.23.cloned.1.call-done = bf16[1,1024,3200]{2,1,0:T(8,128)(2,1)} async-done(((bf16[1,256,3200]{2,1,0:T(8,128)(2,1)}), bf16[1,1024,3200]{2,1,0:T(8,128)(2,1)}) %all-gather.23.cloned.1.call-update) | async-done | bytes 6553616 | tf_op jit(solution)/shard_map/all_gather | solution.py:40
  344.5 37.7 %fusion.55 = f32[4096,3200]{1,0:T(8,128)} fusion(bf16[1,1024,3200]{2,1,0:T(8,128)(2,1)} %all-gather.23.cloned.1.call-done, bf16[4096,1024]{0,1:T(8,128)(2,1)} %get-tuple-element.27, f32[4096]{0:T(1024)S(1)} %fusion.77), kind=kOutput, calls=%fused_computation.87 | convolution fusion | flops 26856128512 | bytes 67387392 | tf_op jit(solution)/shard_map/jvp()/dot_general | solution.py:22
  382.1 28.9 %all-gather.19.cloned.1.call-done = bf16[1,1024,3200]{2,1,0:T(8,128)(2,1)} async-done(((bf16[1,256,3200]{2,1,0:T(8,128)(2,1)}), bf16[1,1024,3200]{2,1,0:T(8,128)(2,1)}) %all-gather.19.cloned.1.call-update) | async-done | bytes 6553616 | tf_op jit(solution)/shard_map/all_gather | solution.py:40
  411.0 69.4 %fusion.2 = (bf16[4096,3200]{1,0:T(8,128)(2,1)}, f32[4096,3200]{1,0:T(8,128)}) fusion(f32[4096,3200]{1,0:T(8,128)} %fusion.55, bf16[4096,3200]{1,0:T(8,128)(2,1)} %convolution_convert_fusion.1, bf16[1,1024,3200]{2,1,0:T(8,128)(2,1)} %all-gather.19.cloned.1.call-done, bf16[4096,1024]{0,1:T(8,128)(2,1)} %get-tuple-element.27, f32[4096]{0:T(1024)S(1)} %fusion.77), kind=kOutput, calls=%fused_computation.8 | convolution fusion | flops 27013414912 | bytes 172244992 | tf_op jit(solution)/shard_map/jvp()/dot_general | solution.py:21
  480.4 35.2 %fusion.59 = bf16[4096,1024]{0,1:T(8,128)(2,1)} fusion(bf16[4096,3200]{1,0:T(8,128)(2,1)} %get-tuple-element.28, bf16[1,1024,3200]{2,1,0:T(8,128)(2,1)} %all-gather.19.cloned.1.call-done), kind=kOutput, calls=%fused_computation.91 | convolution fusion | flops 26843545600 | bytes 41156608 | tf_op jit(solution)/shard_map/transpose(jvp())/dot_general | solution.py:21
  515.6 40.7 %fusion.21 = (f32[4096]{0:T(1024)S(1)}, bf16[4096,1024]{0,1:T(8,128)(2,1)}) fusion(bf16[4096,1024]{0,1:T(8,128)(2,1)} %get-tuple-element.27, bf16[4096,1024]{0,1:T(8,128)(2,1)} %fusion.59, bf16[1,1024,3200]{2,1,0:T(8,128)(2,1)S(1)} %copy-done.17, bf16[4096,3200]{1,0:T(8,128)(2,1)} %convolution_convert_fusion.1, f32[4096,3200]{1,0:T(8,128)} %get-tuple-element.29), kind=kOutput, calls=%fused_computation.39 | convolution fusion | flops 26947350528 | bytes 110379008 | tf_op jit(solution)/shard_map/transpose(jvp())/dot_general | solution.py:22
  568.4 34.2 %convolution_convert_fusion.3 = bf16[3200,1024]{1,0:T(8,128)(2,1)} fusion(bf16[4096,3200]{1,0:T(8,128)(2,1)} %get-tuple-element.24, bf16[4096,1024]{0,1:T(8,128)(2,1)} %fusion.23), kind=kOutput, calls=%fused_computation.68 | convolution fusion | flops 26846822400 | bytes 41156608 | tf_op jit(solution)/shard_map/transpose(jvp())/dot_general | solution.py:10
  602.7 44.1 %fusion.29 = bf16[3200,1024]{1,0:T(8,128)(2,1)} fusion(bf16[1,4096,1024]{2,1,0:T(8,128)(2,1)} %param.12, f32[4096,3200]{1,0:T(8,128)} %fusion.55, f32[4096,3200]{1,0:T(8,128)} %get-tuple-element.29), kind=kOutput, calls=%fused_computation.63 | convolution fusion | flops 26925465600 | bytes 119799808 | tf_op jit(solution)/shard_map/transpose(jvp())/dot_general | solution.py:10
  647.0 35.4 %convolution_convert_fusion = bf16[4096,3200]{1,0:T(8,128)(2,1)} fusion(bf16[4096,1024]{0,1:T(8,128)(2,1)} %fusion.23, bf16[1,3200,1024]{2,1,0:T(8,128)(2,1)} %all-gather.17.cloned.1.call-done), kind=kOutput, calls=%fused_computation.22 | convolution fusion | flops 26856652800 | bytes 41156608 | tf_op jit(solution)/shard_map/transpose(jvp())/dot_general | solution.py:10
  682.4 44.4 %fusion.36 = bf16[1024,3200]{1,0:T(8,128)(2,1)} fusion(bf16[4096,3200]{1,0:T(8,128)(2,1)} %convolution_convert_fusion, f32[4096,3200]{1,0:T(8,128)} %fusion.67, bf16[1,4096,1024]{1,2,0:T(8,128)(2,1)} %copy.20, f32[4096]{0:T(1024)S(1)} %copy-done.16), kind=kOutput, calls=%fused_computation.66 | convolution fusion | flops 26938048512 | bytes 93601792 | tf_op jit(solution)/shard_map/transpose(jvp())/dot_general | solution.py:22
  726.9 44.7 %fusion.32 = bf16[1024,3200]{1,0:T(8,128)(2,1)} fusion(bf16[4096,3200]{1,0:T(8,128)(2,1)} %convolution_convert_fusion.1, bf16[4096,1024]{0,1:T(8,128)(2,1)} %get-tuple-element.27, f32[4096]{0:T(1024)S(1)} %copy-done.11, f32[4096,3200]{1,0:T(8,128)} %get-tuple-element.29), kind=kOutput, calls=%fused_computation.64 | convolution fusion | flops 26938048512 | bytes 93601792 | tf_op jit(solution)/shard_map/transpose(jvp())/dot_general | solution.py:22
  771.8 49.3 %fusion.33 = bf16[1024,3200]{1,0:T(8,128)(2,1)} fusion(f32[4096,3200]{1,0:T(8,128)} %fusion.67, f32[4096,3200]{1,0:T(8,128)} %get-tuple-element.25, bf16[4096,3200]{1,0:T(8,128)(2,1)} %convolution_convert_fusion, bf16[1,4096,1024]{1,2,0:T(8,128)(2,1)} %copy.20, f32[4096]{0:T(1024)S(1)} %copy-done.16), kind=kOutput, calls=%fused_computation.65 | convolution fusion | flops 27003584512 | bytes 146030592 | tf_op jit(solution)/shard_map/transpose(jvp())/dot_general | solution.py:21
  821.2 37.1 %convolution_convert_fusion.2 = bf16[1024,3200]{1,0:T(8,128)(2,1)} fusion(bf16[4096,3200]{1,0:T(8,128)(2,1)} %get-tuple-element.28, bf16[4096,1024]{0,1:T(8,128)(2,1)} %get-tuple-element.27, f32[4096]{0:T(1024)S(1)} %copy-done.12), kind=kOutput, calls=%fused_computation.67 | convolution fusion | flops 26856128512 | bytes 41172992 | tf_op jit(solution)/shard_map/transpose(jvp())/dot_general | solution.py:21
  867.1 56.9 %reduce-scatter.7.cloned.1.call-done = bf16[256,3200]{1,0:T(8,128)(2,1)} async-done(((bf16[1024,3200]{1,0:T(8,128)(2,1)}), bf16[256,3200]{1,0:T(8,128)(2,1)}) %reduce-scatter.7.cloned.1.call-update) | async-done | bytes 1638416 | tf_op jit(solution)/shard_map/reduce_scatter | solution.py:53
  924.0 64.5 %reduce-scatter.9.cloned.1.call-done = bf16[256,3200]{1,0:T(8,128)(2,1)} async-done(((bf16[1024,3200]{1,0:T(8,128)(2,1)}), bf16[256,3200]{1,0:T(8,128)(2,1)}) %reduce-scatter.9.cloned.1.call-update) | async-done | bytes 1638416 | tf_op jit(solution)/shard_map/reduce_scatter | solution.py:53
  1004.5 13.6 %fusion.51 = (bf16[2,800,1024]{2,1,0:T(8,128)(2,1)}, f32[2,800,1024]{2,1,0:T(8,128)}, f32[2,800,1024]{2,1,0:T(8,128)}) fusion(bf16[2,800,1024]{2,1,0:T(8,128)(2,1)S(1)} %copy-done.2, f32[]{:T(128)S(6)} %min_shard_map.3, bf16[1,800,1024]{2,1,0:T(8,128)(2,1)} %bitcast.76, bf16[1,800,1024]{2,1,0:T(8,128)(2,1)} %bitcast.74, f32[2,800,1024]{2,1,0:T(8,128)} %param.21, ...), kind=kLoop, calls=%fused_computation.83 | loop fusion | flops 32768000 | bytes 36044804 | tf_op jit(solution)/shard_map/convert_element_type | solution.py:30
  1019.6 20.4 %fusion.42 = (bf16[2,256,3200]{2,1,0:T(8,128)(2,1)}, f32[2,256,3200]{2,1,0:T(8,128)}, f32[2,256,3200]{2,1,0:T(8,128)}, bf16[2,256,3200]{2,1,0:T(8,128)(2,1)}, f3...) fusion(bf16[2,256,3200]{2,1,0:T(8,128)(2,1)S(1)} %copy-done.3, f32[]{:T(128)S(6)} %min_shard_map.3, ...), kind=kLoop, calls=%fused_computation.74 | loop fusion | flops 65536000 | bytes 72089600 | tf_op jit(solution)/shard_map/convert_element_type | solution.py:30
  (79 shorter events, 85.7 us)
Async XLA Ops:
  7.2 71.0 %all-gather.13.cloned.1.call-start = ((), (), s32[]{:S(2)}) async-start(), calls=%async_computation.12 | async-start | bytes 8192000 | tf_op jit(solution)/shard_map/all_gather | solution.py:40
  11.3 133.5 %all-gather.15.cloned.1.call-start = ((), (), s32[]{:S(2)}) async-start(), calls=%async_computation.13 | async-start | bytes 8192000 | tf_op jit(solution)/shard_map/all_gather | solution.py:40
  15.3 196.2 %all-gather.17.cloned.1.call-start = ((), (), s32[]{:S(2)}) async-start(), calls=%async_computation.14 | async-start | bytes 8192000 | tf_op jit(solution)/shard_map/all_gather | solution.py:40
  17.5 260.5 %all-gather.21.cloned.1.call-start = ((), (), s32[]{:S(2)}) async-start(), calls=%async_computation.16 | async-start | bytes 8192000 | tf_op jit(solution)/shard_map/all_gather | solution.py:40
  18.1 326.3 %all-gather.23.cloned.1.call-start = ((), (), s32[]{:S(2)}) async-start(), calls=%async_computation.17 | async-start | bytes 8192000 | tf_op jit(solution)/shard_map/all_gather | solution.py:40
  18.8 392.2 %all-gather.19.cloned.1.call-start = ((), (), s32[]{:S(2)}) async-start(), calls=%async_computation.15 | async-start | bytes 8192000 | tf_op jit(solution)/shard_map/all_gather | solution.py:40
  19.4 839.0 %reduce-scatter.15.cloned.1.call-start = ((), (), s32[]{:S(2)}) async-start(), calls=%async_computation.10 | async-start | bytes 8192000 | tf_op jit(solution)/shard_map/reduce_scatter | solution.py:53
  36.3 108.6 %copy-start.15 = (f32[4096]{0:T(1024)}, f32[4096]{0:T(1024)S(1)}, u32[]{:S(2)}) copy-start(f32[4096]{0:T(1024)S(1)} %add_rsqrt_fusion) | copy-start | bytes 49156
  248.8 65.6 %copy-start.13 = (f32[4096]{0:T(1024)}, f32[4096]{0:T(1024)S(1)}, u32[]{:S(2)}) copy-start(f32[4096]{0:T(1024)S(1)} %get-tuple-element.26) | copy-start | bytes 49156
  248.8 162.2 %copy-start.9 = (f32[4096]{0:T(1024)}, f32[4096]{0:T(1024)S(1)}, u32[]{:S(2)}) copy-start(f32[4096]{0:T(1024)S(1)} %fusion.77) | copy-start | bytes 49156
  480.4 35.2 %copy-start.17 = (bf16[1,1024,3200]{2,1,0:T(8,128)(2,1)S(1)}, bf16[1,1024,3200]{2,1,0:T(8,128)(2,1)}, u32[]{:S(2)}) copy-start(bf16[1,1024,3200]{2,1,0:T(8,128)(2,1)} %all-gather.23.cloned.1.call-done) | copy-start | bytes 19660804
  515.6 40.7 %copy-start.14 = (f32[4096]{0:T(1024)S(1)}, f32[4096]{0:T(1024)}, u32[]{:S(2)}) copy-start(f32[4096]{0:T(1024)} %copy-done.13) | copy-start | bytes 49156
  515.6 40.8 %copy-start = (bf16[1,4096,1024]{1,2,0:T(8,128)(2,1)S(1)}, bf16[1,4096,1024]{1,2,0:T(8,128)(2,1)}, u32[]{:S(2)}) copy-start(bf16[1,4096,1024]{1,2,0:T(8,128)(2,1)} %copy.21) | copy-start | bytes 25165828
  515.6 40.8 %copy-start.10 = (f32[4096]{0:T(1024)S(1)}, f32[4096]{0:T(1024)}, u32[]{:S(2)}) copy-start(f32[4096]{0:T(1024)} %copy-done.9) | copy-start | bytes 49156
  602.7 255.8 %reduce-scatter.17.cloned.1.call-start = ((), (), s32[]{:S(2)}) async-start(), calls=%async_computation.11 | async-start | bytes 8192000 | tf_op jit(solution)/shard_map/reduce_scatter | solution.py:53
  646.9 35.5 %copy-start.16 = (f32[4096]{0:T(1024)S(1)}, f32[4096]{0:T(1024)}, u32[]{:S(2)}) copy-start(f32[4096]{0:T(1024)} %copy-done.15) | copy-start | bytes 49156
  646.9 215.9 %reduce-scatter.11.cloned.1.call-start = ((), (), s32[]{:S(2)}) async-start(), calls=%async_computation.8 | async-start | bytes 8192000 | tf_op jit(solution)/shard_map/reduce_scatter | solution.py:53
  682.4 44.5 %copy-start.11 = (f32[4096]{0:T(1024)S(1)}, f32[4096]{0:T(1024)}, u32[]{:S(2)}) copy-start(f32[4096]{0:T(1024)} %copy-done.9) | copy-start | bytes 49156
  726.8 136.0 %reduce-scatter.13.cloned.1.call-start = ((), (), s32[]{:S(2)}) async-start(), calls=%async_computation.9 | async-start | bytes 8192000 | tf_op jit(solution)/shard_map/reduce_scatter | solution.py:53
  771.7 152.3 %reduce-scatter.7.cloned.1.call-start = ((), (), s32[]{:S(2)}) async-start(), calls=%async_computation.6 | async-start | bytes 8192000 | tf_op jit(solution)/shard_map/reduce_scatter | solution.py:53
  771.8 49.4 %copy-start.12 = (f32[4096]{0:T(1024)S(1)}, f32[4096]{0:T(1024)}, u32[]{:S(2)}) copy-start(f32[4096]{0:T(1024)} %copy-done.9) | copy-start | bytes 49156
  821.1 167.3 %reduce-scatter.9.cloned.1.call-start = ((), (), s32[]{:S(2)}) async-start(), calls=%async_computation.7 | async-start | bytes 8192000 | tf_op jit(solution)/shard_map/reduce_scatter | solution.py:53
  858.4 146.1 %copy-start.2 = (bf16[2,800,1024]{2,1,0:T(8,128)(2,1)S(1)}, bf16[2,800,1024]{2,1,0:T(8,128)(2,1)}, u32[]{:S(2)}) copy-start(bf16[2,800,1024]{2,1,0:T(8,128)(2,1)} %param.15) | copy-start | bytes 9830404
  1004.5 15.1 %copy-start.8 = (bf16[256,3200]{1,0:T(8,128)(2,1)S(1)}, bf16[256,3200]{1,0:T(8,128)(2,1)}, u32[]{:S(2)}) copy-start(bf16[256,3200]{1,0:T(8,128)(2,1)} %reduce-scatter.9.cloned.1.call-done) | copy-start | bytes 4915204
  (6 other events, 77.3 us)
Sparse Core Ops, SparseCore 0:
  11.5 66.6 all-gather.12
  80.3 64.4 all-gather.14
  147.0 64.4 all-gather.16
  213.5 64.4 all-gather.20
  280.0 64.4 all-gather.22
  346.5 64.4 all-gather.18
  602.8 62.6 reduce-scatter.14
  668.4 61.7 reduce-scatter.16
  733.0 61.7 reduce-scatter.10
  797.5 61.7 reduce-scatter.12
  862.2 61.7 reduce-scatter.6
  926.7 61.7 reduce-scatter.8
where the time goes:
time: 1060 us; the launch traced here: 1050 us
  matrix products  642 us (61%)
  waiting for transfers between devices  279 us (26%)
  other arithmetic  63.9 us (6%)
  local copies, waits for them, and re-layouts  35.1 us (3%)
  between operations  17.3 us (2%)
    dot_general x5, matrix products, layer(): gate = jnp.dot(a, w['w_gate'], preferred_element_type=jnp.float32)  229 us
    dot_general x5, matrix products, layer(): up = jnp.dot(a, w['w_up'], preferred_element_type=jnp.float32)  226 us
    dot_general x5, matrix products, matmul(): jnp.dot(a, w, preferred_element_type=jnp.float32).astype(jnp.bfloat16)  187 us
    all_gather x6, waiting for transfers between devices, fetched(): lax.all_gather(w[number], 'dp', axis=0, tiled=True)  156 us
    reduce_scatter x6, waiting for transfers between devices, step(): lax.psum_scatter(by_w[name], 'dp', scatter_dimension=0, tiled=True)  121 us
    convert_element_type x2, other arithmetic, adamw(): return ((w - 0.02 * step).astype(jnp.bfloat16), m, v)  34 us
    unnamed x38, local copies, waits for them, and re-layouts  25.2 us
  transfers between devices with their start and end apart: 12, of which 8 were waited for; matrix products, arithmetic and copies ran while one was open for 48% of the time, Pallas kernels for 0%

commit v1 on v0

v1 whole, which is shorter than its diff:
```python
import jax
import jax.numpy as jnp
from jax import lax
from jax.experimental import pallas as pl
from jax.experimental.pallas import tpu as pltpu
from jax.sharding import PartitionSpec as P


F32, BF16 = jnp.float32, jnp.bfloat16
ANY = pl.BlockSpec(memory_space=pl.ANY)


def call(kernel, grid, in_specs, out_specs, out_shape, flops, nbytes, scratch=(), aliases=None):
    return pl.pallas_call(
        kernel,
        grid=grid,
        in_specs=in_specs,
        out_specs=out_specs,
        out_shape=out_shape,
        scratch_shapes=scratch,
        input_output_aliases=aliases or {},
        cost_estimate=pl.CostEstimate(flops=flops, bytes_accessed=nbytes, transcendentals=0),
        compiler_params=pltpu.CompilerParams(
            dimension_semantics=("arbitrary",) * len(grid), vmem_limit_bytes=62 * 1024 * 1024
        ),
    )


def rows(bt, width):
    return pl.BlockSpec((bt, width), lambda i: (i, 0))


def cols(height, bt):
    return pl.BlockSpec((height, bt), lambda i: (0, i))


def whole(shape):
    return pl.BlockSpec(shape, lambda *i: (0,) * len(shape), pipeline_mode=pl.Buffered(1))


def sds(shape, dtype):
    return jax.ShapeDtypeStruct(shape, dtype)


def dot(a, b):
    return jnp.dot(a, b, preferred_element_type=F32)


def dot_nt(a, b):
    return lax.dot_general(a, b, (((1,), (1,)), ((), ())), preferred_element_type=F32)


def normed(h):
    wide = h.astype(F32)
    scale = lax.rsqrt(jnp.mean(wide * wide, -1, keepdims=True) + 1e-6)
    return (wide * scale).astype(BF16)


def pieces(f, parts=3):
    step = f // parts // 256 * 256
    return [(i * step, step if i < parts - 1 else f - i * step) for i in range(parts)]


def other_core():
    return lax.axis_index("rep") % 2


class Halves:
    def __init__(self, arrays, starts, count):
        self.arrays, self.starts, self.count = arrays, starts, count
        self.owners, self.height = arrays[0].shape[0], arrays[0].shape[1] // count

    def loads(self, refs, which, o, n, into, sem):
        core = other_core()
        out = []
        for part, start in enumerate(self.starts):
            end = start + self.arrays[2 * part].shape[2]
            low, high = max(o, start), min(o + n, end)
            if low >= high:
                continue
            for ref, side in ((refs[2 * part], core), (refs[2 * part + 1], 1 - core)):
                for owner in range(self.owners):
                    at = pl.multiple_of((2 * owner + side) * self.height, self.height)
                    out.append(
                        pltpu.make_async_copy(
                            ref.at[owner, pl.ds(which * self.height, self.height), pl.ds(low - start, high - low)],
                            into.at[pl.ds(at, self.height), pl.ds(low - o, high - low)],
                            sem.at[len(out)],
                        )
                    )
        return out

    def load_rows(self, refs, o, n, into, sem):
        core = other_core()
        out = []
        for block in range(2 * self.owners):
            start = block * self.height
            low, high = max(o, start), min(o + n, start + self.height)
            if low >= high:
                continue
            both = [
                pltpu.make_async_copy(
                    ref.at[block // 2, pl.ds(low - start, high - low), :], into.at[pl.ds(low - o, high - low), :], sem.at[len(out)]
                )
                for ref in refs
            ]
            pl.when(core == block % 2)(both[0].start)
            pl.when(core != block % 2)(both[1].start)
            out.append(both[0])
        return out


def begin(copies):
    for copy in copies:
        copy.start()
    return copies


def finish(copies):
    for copy in copies:
        copy.wait()


SEM = pltpu.SemaphoreType.DMA((16,))


def prepare(h, dy, bt=512):
    t, d = h.shape

    def kernel(h_ref, dy_ref, a_ref, at_ref, dyt_ref):
        a = normed(h_ref[...])
        a_ref[...] = a
        at_ref[...] = a.T
        dyt_ref[...] = dy_ref[...].T

    return call(
        kernel, (t // bt,), [rows(bt, d)] * 2, [rows(bt, d), cols(d, bt), cols(d, bt)],
        [sds((t, d), BF16), sds((d, t), BF16), sds((d, t), BF16)], 8 * t * d, 10 * t * d,
    )(h, dy)


def up(a, w, cut, bt=256):
    t, d = a.shape
    f = cut[-1][0] + cut[-1][1]
    k, m = len(cut), len(w.arrays)

    def kernel(a_ref, *refs):
        act_ref, *outs = refs[m : m + 1 + 2 * k]
        wg_ref, wu_ref, sem_g, sem_u = refs[m + 1 + 2 * k :]

        @pl.when(pl.program_id(0) == 0)
        def _():
            loads = begin(w.loads(refs[:m], 0, 0, f, wg_ref, sem_g)) + begin(w.loads(refs[:m], 1, 0, f, wu_ref, sem_u))
            finish(loads)

        a = a_ref[...]
        g, u = dot(a, wg_ref[...]), dot(a, wu_ref[...])
        for (o, n), g_ref, u_ref in zip(cut, outs[:k], outs[k:]):
            g_ref[...] = g[:, o : o + n]
            u_ref[...] = u[:, o : o + n]
        act_ref[...] = (g * jax.nn.sigmoid(g) * u).astype(BF16)

    return call(
        kernel, (t // bt,), [rows(bt, d)] + [ANY] * m,
        [rows(bt, f)] + [rows(bt, n) for _, n in cut] * 2,
        [sds((t, f), BF16)] + [sds((t, n), F32) for _, n in cut] * 2,
        4 * t * d * f, 10 * t * f, [pltpu.VMEM((d, f), BF16)] * 2 + [SEM] * 2,
    )(a, *w.arrays)


def down(act, w, h, bt=512):
    t, f = act.shape
    d = h.shape[1]

    def kernel(act_ref, mine, theirs, h_ref, o_ref, a_ref, at_ref, wd_ref, sem):
        @pl.when(pl.program_id(0) == 0)
        def _():
            finish(w.load_rows((mine, theirs), 0, f, wd_ref, sem))

        o = h_ref[...] + dot(act_ref[...], wd_ref[...]).astype(BF16)
        o_ref[...] = o
        a = normed(o)
        a_ref[...] = a
        at_ref[...] = a.T

    return call(
        kernel, (t // bt,), [rows(bt, f), ANY, ANY, rows(bt, d)], [rows(bt, d), rows(bt, d), cols(d, bt)],
        [sds((t, d), BF16), sds((t, d), BF16), sds((d, t), BF16)], 2 * t * d * f, 2 * t * f, [pltpu.VMEM((f, d), BF16), SEM],
    )(act, *w.arrays, h)


def gated_back(g, u, by):
    s = jax.nn.sigmoid(g)
    silu = g * s
    by = by.astype(BF16).astype(F32)
    return ((by * u) * (s * (1.0 + g * (1.0 - s)))).astype(BF16), (by * silu).astype(BF16), (silu * u).astype(BF16)


def last_piece(a, at, dy, dyt, w, w_down, o, n, so_far, bt=512):
    t, d = a.shape
    f = 2 * w_down.owners * w_down.height
    steps, m = t // bt, len(w.arrays)

    def kernel(a_ref, at_ref, dy_ref, dyt_ref, *rest):
        dg_ref, du_ref, up_ref, down_hbm, wg_ref, wu_ref, wd_ref, sum_g, sum_u, sum_d, flipped, sem_g, sem_u, sem = rest[-14:]
        i = pl.program_id(0)

        @pl.when(i == 0)
        def _():
            loads = begin(w.loads(rest[:m], 0, o, n, wg_ref, sem_g)) + begin(w.loads(rest[:m], 1, o, n, wu_ref, sem_u))
            loads += w_down.load_rows(rest[m : m + 2], o, n, wd_ref, sem)
            for total in (sum_g, sum_u, sum_d):
                total[...] = jnp.zeros_like(total)
            finish(loads)

        g, u = dot(a_ref[...], wg_ref[...]), dot(a_ref[...], wu_ref[...])
        dg_ref[...], du_ref[...], act = gated_back(g, u, dot_nt(dy_ref[...], wd_ref[...]))
        sum_d[...] += dot(dyt_ref[...], act)
        sum_g[...] += dot(at_ref[...], dg_ref[...])
        sum_u[...] += dot(at_ref[...], du_ref[...])

        @pl.when(i == steps - 1)
        def _():
            flipped[...] = sum_d[...].astype(BF16).T
            store = pltpu.make_async_copy(flipped, down_hbm.at[pl.ds(o, n), :], sem.at[0])
            store.start()
            up_ref[:, :n] = sum_g[...].astype(BF16)
            up_ref[:, n:] = sum_u[...].astype(BF16)
            store.wait()

    return call(
        kernel, (steps,), [rows(bt, d), cols(d, bt)] * 2 + [ANY] * (m + 2 + len(so_far)),
        [rows(bt, n), rows(bt, n), whole((d, 2 * n)), ANY],
        [sds((t, n), BF16), sds((t, n), BF16), sds((d, 2 * n), BF16), sds((f, d), BF16)],
        12 * t * d * n, 4 * t * n + 8 * t * d,
        [pltpu.VMEM((d, n), BF16)] * 2 + [pltpu.VMEM((n, d), BF16)] + [pltpu.VMEM((d, n), F32)] * 3
        + [pltpu.VMEM((n, d), BF16), SEM, SEM, SEM],
        aliases={6 + m: 3} if so_far else None,
    )(a, at, dy, dyt, *w.arrays, *w_down.arrays, *so_far)


def first_piece(at, g, u, by, w_down, o, bt=512):
    d, t = at.shape
    n = g.shape[1]
    steps = t // bt

    def kernel(at_ref, g_ref, u_ref, by_ref, mine, theirs, up_ref, wd_ref, sum_g, sum_u, sem):
        i = pl.program_id(0)

        @pl.when(i == 0)
        def _():
            loads = w_down.load_rows((mine, theirs), o, n, wd_ref, sem)
            for total in (sum_g, sum_u):
                total[...] = jnp.zeros_like(total)
            finish(loads)

        dg, du, _ = gated_back(g_ref[...], u_ref[...], dot_nt(by_ref[...], wd_ref[...]))
        sum_g[...] += dot(at_ref[...], dg)
        sum_u[...] += dot(at_ref[...], du)

        @pl.when(i == steps - 1)
        def _():
            up_ref[:, :n] = sum_g[...].astype(BF16)
            up_ref[:, n:] = sum_u[...].astype(BF16)

    return call(
        kernel, (steps,), [cols(d, bt), rows(bt, n), rows(bt, n), rows(bt, d), ANY, ANY], whole((d, 2 * n)),
        sds((d, 2 * n), BF16), 6 * t * d * n, 8 * t * n + 4 * t * d,
        [pltpu.VMEM((n, d), BF16)] + [pltpu.VMEM((d, n), F32)] * 2 + [SEM],
    )(at, g, u, by, *w_down.arrays)


def input_back(dgs, dus, w, h, dy, cut, bt=256):
    t, d = h.shape
    f = cut[-1][0] + cut[-1][1]
    k, m = len(cut), len(w.arrays)

    def kernel(*refs):
        h_ref, dy_ref, o_ref, ot_ref, wg_ref, wu_ref, sem_g, sem_u = refs[2 * k + m :]

        @pl.when(pl.program_id(0) == 0)
        def _():
            parts = refs[2 * k : 2 * k + m]
            finish(begin(w.loads(parts, 0, 0, f, wg_ref, sem_g)) + begin(w.loads(parts, 1, 0, f, wu_ref, sem_u)))

        by_g = sum(dot_nt(r[...], wg_ref[:, o : o + n]) for r, (o, n) in zip(refs[:k], cut))
        by_u = sum(dot_nt(r[...], wu_ref[:, o : o + n]) for r, (o, n) in zip(refs[k : 2 * k], cut))
        by = (by_g.astype(BF16) + by_u.astype(BF16)).astype(F32)
        wide = h_ref[...].astype(F32)
        scale = lax.rsqrt(jnp.mean(wide * wide, -1, keepdims=True) + 1e-6)
        along = jnp.mean(by * wide, -1, keepdims=True) * (scale * scale * scale)
        o = dy_ref[...] + (by * scale - wide * along).astype(BF16)
        o_ref[...] = o
        ot_ref[...] = o.T

    return call(
        kernel, (t // bt,), [rows(bt, n) for _, n in cut] * 2 + [ANY] * m + [rows(bt, d)] * 2,
        [rows(bt, d), cols(d, bt)], [sds((t, d), BF16), sds((d, t), BF16)],
        4 * t * d * f, 4 * t * f, [pltpu.VMEM((d, f), BF16)] * 2 + [SEM] * 2,
    )(*dgs, *dus, *w.arrays, h, dy)


def down_grad(byt, act, bn=640):
    d, t = byt.shape
    f = act.shape[1]

    def kernel(l_ref, r_ref, o_ref):
        o_ref[...] = dot(l_ref[...], r_ref[...]).astype(BF16).T

    return call(
        kernel, (f // bn,), [whole((d, t)), cols(t, bn)], rows(bn, d), sds((f, d), BF16),
        2 * t * d * f, 2 * t * f + 2 * t * d,
    )(byt, act)


def adamw(w, m, v, g):
    m = 0.9 * m + 0.1 * g
    v = 0.95 * v + 0.05 * g * g
    step = m * lax.rsqrt(v + 1e-8) + 0.1 * w
    return (w - 0.02 * step).astype(BF16), m, v


def update(ws, ms, vs, grads, factor, runs, br):
    layers, height, width = ws[0].shape
    k, count = len(ws), sum(len(g) for g in grads)
    first = [sum(len(g) for g in grads[:l]) for l in range(layers)]

    def kernel(*refs):
        factor_ref = refs[0]
        w_refs, m_refs, v_refs = (refs[1 + i * k : 1 + (i + 1) * k] for i in range(3))
        g_refs = refs[1 + 3 * k : 1 + 3 * k + count]
        outs = refs[1 + 3 * k + count :]
        scale = factor_ref[0, 0]
        for l in range(layers):

            @pl.when(pl.program_id(0) == l)
            def _():
                for i in range(k):
                    for array, source, to, n in runs[l][i]:
                        s = slice(to, to + n)
                        g = g_refs[first[l] + array][:, source : source + n].astype(F32) * scale
                        outs[i][0, :, s], outs[k + i][0, :, s], outs[2 * k + i][0, :, s] = adamw(
                            w_refs[i][0, :, s].astype(F32), m_refs[i][0, :, s], v_refs[i][0, :, s], g
                        )

    block = pl.BlockSpec((1, br, width), lambda l, i: (l, i, 0))
    steps = height // br

    def of(l):
        return lambda at, i: (jnp.where(at == l, i, jnp.where(at < l, 0, steps - 1)), 0)

    size = layers * height * width
    return call(
        kernel, (layers, steps),
        [pl.BlockSpec(memory_space=pltpu.SMEM)] + [block] * (3 * k)
        + [pl.BlockSpec((br, g.shape[1]), of(l)) for l in range(layers) for g in grads[l]],
        [block] * (3 * k),
        [sds(w.shape, BF16) for w in ws] + [sds(w.shape, F32) for w in ws] * 2,
        20 * k * size, 24 * k * size,
    )(factor, *ws, *ms, *vs, *(g for l in grads for g in l))


def solution(mesh):
    reps = mesh.shape["rep"]
    pairs = [(i, i ^ 1) for i in range(reps)]

    def step(x, dy, *arrays):
        weights, m, v = (arrays[i : i + 3] for i in (0, 3, 6))
        core = lax.axis_index("rep") % 2

        def fetched(shards, columns=slice(None)):
            halves = [lax.dynamic_slice_in_dim(w[:, columns], core * (w.shape[0] // 2), w.shape[0] // 2, 0) for w in shards]
            half = halves[0] if len(halves) == 1 else jnp.concatenate(halves)
            mine = lax.all_gather(half, "dp", axis=0, tiled=False)
            return [mine, lax.ppermute(mine, "rep", pairs)]

        def scattered(g):
            return lax.psum_scatter(g, "dp", scatter_dimension=0, tiled=True)

        def squares(gs):
            return sum(jnp.sum(g.astype(F32) ** 2) for g in gs)

        x, dy = x[0], dy[0]
        cut0, cut1 = pieces(weights[0].shape[2], 2), pieces(weights[0].shape[2], 3)
        k0 = len(cut0)
        edge = cut1[1][0]
        gu0 = Halves(fetched([weights[0][0], weights[1][0]]), [0], 2)
        d0 = Halves(fetched([weights[2][0]]), [0], 1)
        d1 = Halves(fetched([weights[2][1]]), [0], 1)
        first = fetched([weights[0][1], weights[1][1]], slice(0, edge))
        rest = fetched([weights[0][1], weights[1][1]], slice(edge, None))
        gu1 = Halves(first + rest, [0, edge], 2)

        a0, a0t, dyt = prepare(x, dy)
        act0, *gu = up(a0, gu0, cut0)
        h1, a1, a1t = down(act0, d0, x)
        dgs, dus, up1, so_far = [], [], [], []
        for o, n in cut1:
            w = Halves(first, [0], 2) if o + n <= edge else Halves(rest, [edge], 2)
            dg, du, g, so_far = last_piece(a1, a1t, dy, dyt, w, d1, o, n, so_far)
            so_far = [so_far]
            dgs.append(dg)
            dus.append(du)
            up1.append(scattered(g))
        down1 = scattered(so_far[0])
        by, byt = input_back(dgs, dus, gu1, h1, dy, cut1)
        down0 = scattered(down_grad(byt, act0))
        up0 = [scattered(first_piece(a0t, gu[j], gu[k0 + j], by, d0, o)) for j, (o, n) in enumerate(cut0)]

        total = lax.psum(squares(up1) + squares([down1]) + squares([down0]) + squares(up0), "dp")
        count = lax.psum(1, "dp") * sum(w.size for w in weights)
        factor = jnp.minimum(1.0, 0.5 * lax.rsqrt(total / count + 1e-30)).reshape(1, 1)
        runs = [[[(j, i * n, o, n) for j, (o, n) in enumerate(cut)] for i in range(2)] for cut in (cut0, cut1)]
        new_up = update(weights[:2], m[:2], v[:2], [up0, up1], factor, runs, weights[0].shape[1] // 4)
        width = weights[2].shape[2]
        whole_run = [[(0, 0, 0, width)]]
        new_down = update(weights[2:], m[2:], v[2:], [[down0], [down1]], factor, [whole_run] * 2, weights[2].shape[1] // 5)
        return tuple(o for i in range(3) for o in (new_up[2 * i], new_up[2 * i + 1], new_down[i]))

    states, cut = P(("rep", "dp"), None, None), P(None, "dp", None)
    return jax.shard_map(
        step,
        mesh=mesh,
        in_specs=(states, states) + (cut,) * 9,
        out_specs=(P("rep", "dp", None),) * 9,
        check_vma=False,
    )
```

time: 1060 us -> 1020 us (0.962)
  matrix products: 642 us -> 0 us
  Pallas kernels: 0 us -> 614 us
  waiting for transfers between devices: 279 us -> 328 us
  other arithmetic: 63.9 us -> 21.9 us
  local copies, waits for them, and re-layouts: 35.1 us -> 14.8 us
    dot_general x15 -> x0, matrix products: 642 us -> none  [the longest x5 229 us: layer(): gate = jnp.dot(a, w['w_gate'], preferred_element_type=jnp.float32)]
    pallas_call x0 -> x12, Pallas kernels: none -> 614 us  [the longest x3 215 us: last_piece(): call(kernel, (steps,), [rows(bt, d), cols(d, bt)] * 2 + [ANY] * (m + 2 +...]
    all_gather x6 -> x5, waiting for transfers between devices: 156 us -> 195 us  [fetched(): mine = lax.all_gather(half, 'dp', axis=0, tiled=False)]
    convert_element_type x2 -> x0, other arithmetic: 34 us -> none  [adamw(): return ((w - 0.02 * step).astype(jnp.bfloat16), m, v)]
    unnamed x38 -> x8, local copies, waits for them, and re-layouts: 25.2 us -> 0.02 us
    add_any x1 -> x0, other arithmetic: 12 us -> none  [normed(): wide = h.astype(jnp.float32)]
    reduce_scatter x6 -> x7, waiting for transfers between devices: 121 us -> 132 us  [scattered(): return lax.psum_scatter(g, 'dp', scatter_dimension=0, tiled=True)]
  transfers between devices with their start and end apart: 12 -> 17, of which waited for: 8 -> 8; matrix products, arithmetic and copies ran while one was open for 48% -> 2% of each run, Pallas kernels for 0% -> 57%
where the time goes in v1:
time: 1020 us; the launch traced here: 1010 us
  Pallas kernels  614 us (60%)
  waiting for transfers between devices  328 us (32%)
  other arithmetic  21.9 us (2%)
  between operations  20.2 us (2%)
  local copies, waits for them, and re-layouts  14.8 us (1%)
    pallas_call x3, Pallas kernels, last_piece(): call(kernel, (steps,), [rows(bt, d), cols(d, bt)] * 2 + [ANY] * (m + 2 +...  215 us
    all_gather x5, waiting for transfers between devices, fetched(): mine = lax.all_gather(half, 'dp', axis=0, tiled=False)  195 us
    reduce_scatter x7, waiting for transfers between devices, scattered(): return lax.psum_scatter(g, 'dp', scatter_dimension=0, tiled=True)  132 us
    pallas_call x2, Pallas kernels, first_piece(): call(kernel, (steps,), [cols(d, bt), rows(bt, n), rows(bt, n), rows(bt, d...  116 us
    pallas_call x1, Pallas kernels, input_back(): call(kernel, (t // bt,), [rows(bt, n) for _, n in cut] * 2 + [ANY] * m +...  74.6 us
    pallas_call x1, Pallas kernels, up(): call(kernel, (t // bt,), [rows(bt, d)] + [ANY] * m, [rows(bt, f)] + [rows...  68.8 us
    pallas_call x2, Pallas kernels, update(): call(kernel, (layers, steps), [pl.BlockSpec(memory_space=pltpu.SMEM)] + [...  41.5 us
    pallas_call x1, Pallas kernels, down_grad(): call(kernel, (f // bn,), [whole((d, t)), cols(t, bn)], rows(bn, d), sds((...  40.9 us
  transfers between devices with their start and end apart: 17, of which 8 were waited for; matrix products, arithmetic and copies ran while one was open for 2% of the time, Pallas kernels for 57%

profile of v1, /device:TPU:112, one launch (start us, length us, event | category | flops | bytes accessed | tf_op | source)
XLA Modules:
  0.0 1009.7 jit_solution(4140974062147603674)
XLA Ops:
  7.3 4.0 slice_bitcast_fusion
  26.0 56.8 %all-gather.13.cloned.1.call-done = bf16[1024,3200]{1,0:T(8,128)(2,1)} async-done(((bf16[256,3200]{1,0:T(8,128)(2,1)}), bf16[1024,3200]{1,0:T(8,128)(2,1)}) %all-gather.13.cloned.1.call-update) | async-done | bytes 6553616 | tf_op jit(solution)/shard_map/all_gather | solution.py:374
  82.8 17.2 %shard_map.178 = (bf16[4096,1024]{1,0:T(8,128)(2,1)}, bf16[1024,4096]{1,0:T(8,128)(2,1)}, bf16[1024,4096]{1,0:T(8,128)(2,1)}) custom-call(bf16[4096,1024]{1,0:T(8,128)(2,1)} %bitcast.14, bf16[4096,1024]{1,0:T(8,128)(2,1)} %bitcast.16), custom_call_target="tpu_custom_call" | custom-call | flops 33554432 | bytes 41943040 | tf_op jit(solution)/shard_map/pallas_call | solution.py:136
  100.1 12.3 %all-gather.15.cloned.1.call-done = bf16[1024,1024]{1,0:T(8,128)(2,1)} async-done(((bf16[256,1024]{1,0:T(8,128)(2,1)}), bf16[1024,1024]{1,0:T(8,128)(2,1)}) %all-gather.15.cloned.1.call-update) | async-done | bytes 2097168 | tf_op jit(solution)/shard_map/all_gather | solution.py:374
  112.4 38.7 %all-gather.9.cloned.1.call-done.mine = bf16[4,400,1024]{2,1,0:T(8,128)(2,1)} async-done(((bf16[1,400,1024]{2,1,0:T(8,128)(2,1)}), bf16[4,400,1024]{2,1,0:T(8,128)(2,1)}) %all-gather.9.cloned.1.call-update) | async-done | bytes 3276816 | tf_op jit(solution)/shard_map/all_gather | solution.py:374
  151.0 38.7 %all-gather.11.cloned.1.call-done.rest_2_ = bf16[4,400,1024]{2,1,0:T(8,128)(2,1)} async-done(((bf16[1,400,1024]{2,1,0:T(8,128)(2,1)}), bf16[4,400,1024]{2,1,0:T(8,128)(2,1)}) %all-gather.11.cloned.1.call-update) | async-done | bytes 3276816 | tf_op jit(solution)/shard_map/all_gather | solution.py:374
  189.7 48.5 %all-gather.17.cloned.1.call-done = bf16[1024,2176]{1,0:T(8,128)(2,1)} async-done(((bf16[256,2176]{1,0:T(8,128)(2,1)}), bf16[1024,2176]{1,0:T(8,128)(2,1)}) %all-gather.17.cloned.1.call-update) | async-done | bytes 4456464 | tf_op jit(solution)/shard_map/all_gather | solution.py:374
  238.2 68.8 %shard_map.179 = (bf16[4096,3200]{1,0:T(8,128)(2,1)}, f32[4096,1536]{1,0:T(8,128)}, f32[4096,1664]{1,0:T(8,128)}, f32[4096,1536]{1,0:T(8,128)}, f32[4096,1664]{1,0:T(8,128)}) custom-call(bf16[4096,1024]{1,0:T(8,128)(2,1)} %get-tuple-element.43.a_ref, bf16[4,256,3200]{2,1,0:T(8,128)(2,1)} %bitcast.22, bf16[4,256,3200]{2,1,0:T(8,128)(2,1)} %collective-permute-done.refs_1_), custom_call_target="tpu_custom_call" | custom-call | flops 53687091200 | bytes 131072000 | tf_op jit(solution)/shard_map/pallas_call | solution.py:163
  307.0 40.6 %shard_map.180 = (bf16[4096,1024]{1,0:T(8,128)(2,1)}, bf16[4096,1024]{1,0:T(8,128)(2,1)}, bf16[1024,4096]{1,0:T(8,128)(2,1)}) custom-call(bf16[4096,3200]{1,0:T(8,128)(2,1)} %get-tuple-element.44.act_ref.r_ref, bf16[4,400,1024]{2,1,0:T(8,128)(2,1)} %all-gather.9.cloned.1.call-done.mine, bf16[4,400,1024]{2,1,0:T(8,128)(2,1)} %collective-permute-done.1.theirs, ...), custom_call_target="tpu_custom_call" | custom-call | flops 26843545600 | bytes 26214400 | tf_op jit(solution)/shard_map/pallas_call | solution.py:186
  347.6 66.6 %shard_map.181 = (bf16[4096,1024]{1,0:T(8,128)(2,1)}, bf16[4096,1024]{1,0:T(8,128)(2,1)}, bf16[1024,2048]{1,0:T(8,128)(2,1)}, bf16[3200,1024]{1,0:T(8,128)(2,1)}) custom-call(bf16[4096,1024]{1,0:T(8,128)(2,1)} %get-tuple-element.45.a_ref, bf16[1024,4096]{1,0:T(8,128)(2,1)} %get-tuple-element.46.at_ref, bf16[4096,1024]{1,0:T(8,128)(2,1)} %bitcast.17, ...), custom_call_target="tpu_custom_call" | custom-call | flops 51539607552 | bytes 50331648 | tf_op jit(solution)/shard_map/pallas_call | solution.py:231
  414.3 67.3 %shard_map.182 = (bf16[4096,1024]{1,0:T(8,128)(2,1)}, bf16[4096,1024]{1,0:T(8,128)(2,1)}, bf16[1024,2048]{1,0:T(8,128)(2,1)}, bf16[3200,1024]{1,0:T(8,128)(2,1)}) custom-call(bf16[4096,1024]{1,0:T(8,128)(2,1)} %get-tuple-element.45.a_ref, bf16[1024,4096]{1,0:T(8,128)(2,1)} %get-tuple-element.46.at_ref, ...), custom_call_target="tpu_custom_call", output_to_operand_aliasing={{3}: (8, {})} | custom-call | flops 51539607552 | bytes 50331648 | tf_op jit(solution)/shard_map/pallas_call | solution.py:231
  481.8 81.1 %shard_map.183 = (bf16[4096,1152]{1,0:T(8,128)(2,1)}, bf16[4096,1152]{1,0:T(8,128)(2,1)}, bf16[1024,2304]{1,0:T(8,128)(2,1)}, bf16[3200,1024]{1,0:T(8,128)(2,1)}) custom-call(bf16[4096,1024]{1,0:T(8,128)(2,1)} %get-tuple-element.45.a_ref, bf16[1024,4096]{1,0:T(8,128)(2,1)} %get-tuple-element.46.at_ref, ...), custom_call_target="tpu_custom_call", output_to_operand_aliasing={{3}: (8, {})} | custom-call | flops 57982058496 | bytes 52428800 | tf_op jit(solution)/shard_map/pallas_call | solution.py:231
  563.0 74.6 %shard_map.184 = (bf16[4096,1024]{1,0:T(8,128)(2,1)}, bf16[1024,4096]{1,0:T(8,128)(2,1)}) custom-call(bf16[4096,1024]{1,0:T(8,128)(2,1)} %get-tuple-element.54.refs_0_, bf16[4096,1024]{1,0:T(8,128)(2,1)} %get-tuple-element.55.refs_1_, bf16[4096,1152]{1,0:T(8,128)(2,1)} %get-tuple-element.56.refs_2_, bf16[4096,1024]{1,0:T(8,128)(2,1)} %get-tuple-element.57.refs_3_, ...), custom_call_target="tpu_custom_call" | custom-call | flops 53687091200 | bytes 52428800 | tf_op jit(solution)/shard_map/pallas_call | solution.py:296
  637.6 54.3 %shard_map.186 = bf16[1024,3072]{1,0:T(8,128)(2,1)} custom-call(bf16[1024,4096]{1,0:T(8,128)(2,1)} %get-tuple-element.62.at_ref, f32[4096,1536]{1,0:T(8,128)} %get-tuple-element.63.g_ref, f32[4096,1536]{1,0:T(8,128)} %get-tuple-element.64.u_ref, bf16[4096,1024]{1,0:T(8,128)(2,1)} %get-tuple-element.65.by_ref, ...), custom_call_target="tpu_custom_call" | custom-call | flops 38654705664 | bytes 67108864 | tf_op jit(solution)/shard_map/pallas_call | solution.py:266
  692.7 40.9 %shard_map.185 = bf16[3200,1024]{1,0:T(8,128)(2,1)} custom-call(bf16[1024,4096]{1,0:T(8,128)(2,1)} %get-tuple-element.61.l_ref, bf16[4096,3200]{1,0:T(8,128)(2,1)} %get-tuple-element.44.act_ref.r_ref), custom_call_target="tpu_custom_call" | custom-call | flops 26843545600 | bytes 34603008 | tf_op jit(solution)/shard_map/pallas_call | solution.py:310
  733.7 61.6 %shard_map.187 = bf16[1024,3328]{1,0:T(8,128)(2,1)} custom-call(bf16[1024,4096]{1,0:T(8,128)(2,1)} %get-tuple-element.62.at_ref, f32[4096,1664]{1,0:T(8,128)} %get-tuple-element.66.g_ref, f32[4096,1664]{1,0:T(8,128)} %get-tuple-element.67.u_ref, bf16[4096,1024]{1,0:T(8,128)(2,1)} %get-tuple-element.65.by_ref, ...), custom_call_target="tpu_custom_call" | custom-call | flops 41875931136 | bytes 71303168 | tf_op jit(solution)/shard_map/pallas_call | solution.py:266
  807.5 8.3 reduce-scatter.14.cloned.1.call-done.refs_5_
  819.3 61.1 %reduce-scatter.16.cloned.1.call-done.refs_4_ = bf16[800,1024]{1,0:T(8,128)(2,1)} async-done(((bf16[3200,1024]{1,0:T(8,128)(2,1)}), bf16[800,1024]{1,0:T(8,128)(2,1)}) %reduce-scatter.16.cloned.1.call-update) | async-done | bytes 1638416 | tf_op jit(solution)/shard_map/reduce_scatter | solution.py:378
  880.4 2.9 multiply_reduce_fusion.1
  883.9 62.5 %reduce-scatter.20.cloned.1.call-done.refs_8_ = bf16[256,3328]{1,0:T(8,128)(2,1)} async-done(((bf16[1024,3328]{1,0:T(8,128)(2,1)}), bf16[256,3328]{1,0:T(8,128)(2,1)}) %reduce-scatter.20.cloned.1.call-update) | async-done | bytes 1703952 | tf_op jit(solution)/shard_map/reduce_scatter | solution.py:378
  946.5 2.9 multiply_reduce_fusion
  950.7 9.4 psum.7
  960.8 16.1 %shard_map.189 = (bf16[2,800,1024]{2,1,0:T(8,128)(2,1)}, f32[2,800,1024]{2,1,0:T(8,128)}, f32[2,800,1024]{2,1,0:T(8,128)}) custom-call(f32[1,1]{1,0:T(1,128)} %bitcast.9.refs_0_, bf16[2,800,1024]{2,1,0:T(8,128)(2,1)} %refs_1_.3, f32[2,800,1024]{2,1,0:T(8,128)} %refs_2_.3, f32[2,800,1024]{2,1,0:T(8,128)} %refs_3_.3, ...), custom_call_target="tpu_custom_call" | custom-call | flops 32768000 | bytes 39321600 | tf_op jit(solution)/shard_map/pallas_call | solution.py:353
  976.9 25.4 %shard_map.188 = (bf16[2,256,3200]{2,1,0:T(8,128)(2,1)}, bf16[2,256,3200]{2,1,0:T(8,128)(2,1)}, f32[2,256,3200]{2,1,0:T(8,128)}, f32[2,256,3200]{2,1,0:T(8,128)}...) custom-call(f32[1,1]{1,0:T(1,128)} %bitcast.9.refs_0_, bf16[2,256,3200]{2,1,0:T(8,128)(2,1)} %refs_1_.2, ...), custom_call_target="tpu_custom_call" | custom-call | flops 65536000 | bytes 78643200 | tf_op jit(solution)/shard_map/pallas_call | solution.py:353
  (65 shorter events, 29.0 us)
Async XLA Ops:
  7.2 75.7 %all-gather.13.cloned.1.call-start = ((), (), s32[]{:S(2)}) async-start(), calls=%async_computation.16 | async-start | bytes 8192000 | tf_op jit(solution)/shard_map/all_gather | solution.py:374
  7.3 4.0 copy-start.1
  16.0 3.5 copy-start
  16.1 96.3 %all-gather.15.cloned.1.call-start = ((), (), s32[]{:S(2)}) async-start(), calls=%async_computation.17 | async-start | bytes 2621440 | tf_op jit(solution)/shard_map/all_gather | solution.py:374
  19.4 131.6 %all-gather.9.cloned.1.call-start = ((), (), s32[]{:S(2)}) async-start(), calls=%async_computation.7 | async-start | bytes 4096000 | tf_op jit(solution)/shard_map/all_gather | solution.py:374
  21.0 3.6 copy-start.2
  21.0 3.7 copy-start.3
  22.0 167.7 %all-gather.11.cloned.1.call-start = ((), (), s32[]{:S(2)}) async-start(), calls=%async_computation.8 | async-start | bytes 4096000 | tf_op jit(solution)/shard_map/all_gather | solution.py:374
  24.5 213.7 %all-gather.17.cloned.1.call-start = ((), (), s32[]{:S(2)}) async-start(), calls=%async_computation.18 | async-start | bytes 5570560 | tf_op jit(solution)/shard_map/all_gather | solution.py:374
  26.0 769.4 %reduce-scatter.8.cloned.1.call-start = ((), (), s32[]{:S(2)}) async-start(), calls=%async_computation.9 | async-start | bytes 5242880 | tf_op jit(solution)/shard_map/reduce_scatter | solution.py:378
  82.8 155.3 %collective-permute-start = (bf16[4,256,3200]{2,1,0:T(8,128)(2,1)}, bf16[4,256,3200]{2,1,0:T(8,128)(2,1)}, u32[]{:S(2)}, u32[]{:S(2)}) collective-permute-start(bf16[4,256,3200]{2,1,0:T(8,128)(2,1)} %bitcast.21), channel_id=1, source_target_pairs={{0,4},{4,0},{8,12},{12,8},{1,5},{5,1},{9,13},{13,9},{2,6},{6,2},{1... | collective-permute-start | bytes 19660808 | tf_op jit(solution)/shard_map/ppermute | solution.py:375
  112.3 235.2 %collective-permute-start.2 = (bf16[4,256,1024]{2,1,0:T(8,128)(2,1)}, bf16[4,256,1024]{2,1,0:T(8,128)(2,1)}, u32[]{:S(2)}, u32[]{:S(2)}) collective-permute-start(bf16[4,256,1024]{2,1,0:T(8,128)(2,1)} %bitcast.27), channel_id=1, source_target_pairs={{0,4},{4,0},{8,12},{12,8},{1,5},{5,1},{9,13},{13,9},{2,6},{6,2},{1... | collective-permute-start | bytes 6291464 | tf_op jit(solution)/shard_map/ppermute | solution.py:375
  151.0 155.9 %collective-permute-start.1 = (bf16[4,400,1024]{2,1,0:T(8,128)(2,1)}, bf16[4,400,1024]{2,1,0:T(8,128)(2,1)}, u32[]{:S(2)}, u32[]{:S(2)}) collective-permute-start(bf16[4,400,1024]{2,1,0:T(8,128)(2,1)} %all-gather.9.cloned.1.call-done.mine), channel_id=1, source_target_pairs={{0,4},{4,0},{8,12},{12,8},{1,5},{5,1},{9,13},{13,9},{2,6},{6,2},{1... | collective-permute-start | bytes 9830408 | tf_op jit(solution)/shard_map/ppermute | solution.py:375
  189.7 157.9 %collective-permute-start.3 = (bf16[4,400,1024]{2,1,0:T(8,128)(2,1)}, bf16[4,400,1024]{2,1,0:T(8,128)(2,1)}, u32[]{:S(2)}, u32[]{:S(2)}) collective-permute-start(bf16[4,400,1024]{2,1,0:T(8,128)(2,1)} %all-gather.11.cloned.1.call-done.rest_2_), channel_id=1, source_target_pairs={{0,4},{4,0},{8,12},{12,8},{1,5},{5,1},{9,13},{13,9},{2,6},{6,2},{1... | collective-permute-start | bytes 9830408 | tf_op jit(solution)/shard_map/ppermute | solution.py:375
  238.2 176.2 %collective-permute-start.4 = (bf16[4,256,2176]{2,1,0:T(8,128)(2,1)}, bf16[4,256,2176]{2,1,0:T(8,128)(2,1)}, u32[]{:S(2)}, u32[]{:S(2)}) collective-permute-start(bf16[4,256,2176]{2,1,0:T(8,128)(2,1)} %bitcast.23), channel_id=1, source_target_pairs={{0,4},{4,0},{8,12},{12,8},{1,5},{5,1},{9,13},{13,9},{2,6},{6,2},{1... | collective-permute-start | bytes 13369352 | tf_op jit(solution)/shard_map/ppermute | solution.py:375
  414.3 383.5 %reduce-scatter.10.cloned.1.call-start = ((), (), s32[]{:S(2)}) async-start(), calls=%async_computation.10 | async-start | bytes 5242880 | tf_op jit(solution)/shard_map/reduce_scatter | solution.py:378
  481.7 319.8 %reduce-scatter.12.cloned.1.call-start = ((), (), s32[]{:S(2)}) async-start(), calls=%async_computation.11 | async-start | bytes 5898240 | tf_op jit(solution)/shard_map/reduce_scatter | solution.py:378
  562.9 241.7 %reduce-scatter.18.cloned.1.call-start = ((), (), s32[]{:S(2)}) async-start(), calls=%async_computation.14 | async-start | bytes 7864320 | tf_op jit(solution)/shard_map/reduce_scatter | solution.py:378
  692.0 123.8 %reduce-scatter.14.cloned.1.call-start = ((), (), s32[]{:S(2)}) async-start(), calls=%async_computation.12 | async-start | bytes 8192000 | tf_op jit(solution)/shard_map/reduce_scatter | solution.py:378
  692.6 187.8 %reduce-scatter.16.cloned.1.call-start = ((), (), s32[]{:S(2)}) async-start(), calls=%async_computation.13 | async-start | bytes 8192000 | tf_op jit(solution)/shard_map/reduce_scatter | solution.py:378
  733.6 212.8 %reduce-scatter.20.cloned.1.call-start = ((), (), s32[]{:S(2)}) async-start(), calls=%async_computation.15 | async-start | bytes 8519680 | tf_op jit(solution)/shard_map/reduce_scatter | solution.py:378
Sparse Core Ops, SparseCore 0:
  16.2 66.6 all-gather.12
  85.0 27.3 all-gather.14
  114.5 36.4 all-gather.8
  153.0 36.6 all-gather.10
  191.7 46.4 all-gather.16
  414.4 43.2 reduce-scatter.7
  481.8 42.6 reduce-scatter.9
  563.1 46.2 reduce-scatter.11
  692.1 59.1 reduce-scatter.17
  754.0 61.7 reduce-scatter.13
  818.6 61.7 reduce-scatter.15
  882.5 63.8 reduce-scatter.19

commit v2 on v1

--- a/solution.py
+++ b/solution.py
@@ -7,10 +7,11 @@
 
 
 F32, BF16 = jnp.float32, jnp.bfloat16
+MIB = 62
 ANY = pl.BlockSpec(memory_space=pl.ANY)
 
 
-def call(kernel, grid, in_specs, out_specs, out_shape, flops, nbytes, scratch=(), aliases=None):
+def call(kernel, grid, in_specs, out_specs, out_shape, flops, nbytes, scratch=(), aliases=None, mib=62):
     return pl.pallas_call(
         kernel,
         grid=grid,
@@ -21,7 +22,7 @@
         input_output_aliases=aliases or {},
         cost_estimate=pl.CostEstimate(flops=flops, bytes_accessed=nbytes, transcendentals=0),
         compiler_params=pltpu.CompilerParams(
-            dimension_semantics=("arbitrary",) * len(grid), vmem_limit_bytes=62 * 1024 * 1024
+            dimension_semantics=("arbitrary",) * len(grid), vmem_limit_bytes=mib * 1024 * 1024
         ),
     )
 
@@ -48,6 +49,10 @@
 
 def dot_nt(a, b):
     return lax.dot_general(a, b, (((1,), (1,)), ((), ())), preferred_element_type=F32)
+
+
+def dot_tn(a, b):
+    return lax.dot_general(a, b, (((0,), (0,)), ((), ())), preferred_element_type=F32)
 
 
 def normed(h):
@@ -56,9 +61,9 @@
     return (wide * scale).astype(BF16)
 
 
-def pieces(f, parts=3):
-    step = f // parts // 256 * 256
-    return [(i * step, step if i < parts - 1 else f - i * step) for i in range(parts)]
+def pieces(f, shares):
+    ends = [f * sum(shares[:i]) // sum(shares) for i in range(len(shares) + 1)]
+    return [(low, high - low) for low, high in zip(ends, ends[1:])]
 
 
 def other_core():
@@ -66,9 +71,9 @@
 
 
 class Halves:
-    def __init__(self, arrays, starts, count):
-        self.arrays, self.starts, self.count = arrays, starts, count
-        self.owners, self.height = arrays[0].shape[0], arrays[0].shape[1] // count
+    def __init__(self, arrays, starts, height, bases=None):
+        self.arrays, self.starts, self.height = arrays, starts, height
+        self.owners, self.bases = arrays[0].shape[0], bases or [0] * len(starts)
 
     def loads(self, refs, which, o, n, into, sem):
         core = other_core()
@@ -83,7 +88,7 @@
                     at = pl.multiple_of((2 * owner + side) * self.height, self.height)
                     out.append(
                         pltpu.make_async_copy(
-                            ref.at[owner, pl.ds(which * self.height, self.height), pl.ds(low - start, high - low)],
+                            ref.at[owner, pl.ds(self.bases[part] + which * self.height, self.height), pl.ds(low - start, high - low)],
                             into.at[pl.ds(at, self.height), pl.ds(low - o, high - low)],
                             sem.at[len(out)],
                         )
@@ -124,6 +129,28 @@
 SEM = pltpu.SemaphoreType.DMA((16,))
 
 
+def halve(wanted):
+    entries = [e for some in wanted for e in some]
+    shapes = [(sum(w.shape[1] // 2 for w, *_ in some), some[0][3]) for some in wanted]
+
+    def kernel(*refs):
+        ins, outs, sem = refs[: len(entries)], refs[len(entries) : -1], refs[-1]
+        copies = []
+        for some, out in zip(wanted, outs):
+            at = 0
+            for w, layer, o, n in some:
+                h = w.shape[1] // 2
+                source = ins[len(copies)].at[layer, pl.ds(pl.multiple_of(other_core() * h, h), h), pl.ds(o, n)]
+                copies.append(pltpu.make_async_copy(source, out.at[pl.ds(at, h), :], sem.at[len(copies)]))
+                at += h
+        finish(begin(copies))
+
+    return call(
+        kernel, (1,), [ANY] * len(entries), [whole(s) for s in shapes], [sds(s, BF16) for s in shapes],
+        1000000, 4 * sum(a * b for a, b in shapes), [SEM],
+    )(*(e[0] for e in entries))
+
+
 def prepare(h, dy, bt=512):
     t, d = h.shape
 
@@ -139,54 +166,51 @@
     )(h, dy)
 
 
-def up(a, w, cut, bt=256):
+def up(a, w, o, n, bt=256):
     t, d = a.shape
-    f = cut[-1][0] + cut[-1][1]
-    k, m = len(cut), len(w.arrays)
+    m = len(w.arrays)
 
     def kernel(a_ref, *refs):
-        act_ref, *outs = refs[m : m + 1 + 2 * k]
-        wg_ref, wu_ref, sem_g, sem_u = refs[m + 1 + 2 * k :]
+        act_ref, g_ref, u_ref, wg_ref, wu_ref, sem_g, sem_u = refs[m:]
 
         @pl.when(pl.program_id(0) == 0)
         def _():
-            loads = begin(w.loads(refs[:m], 0, 0, f, wg_ref, sem_g)) + begin(w.loads(refs[:m], 1, 0, f, wu_ref, sem_u))
-            finish(loads)
-
-        a = a_ref[...]
-        g, u = dot(a, wg_ref[...]), dot(a, wu_ref[...])
-        for (o, n), g_ref, u_ref in zip(cut, outs[:k], outs[k:]):
-            g_ref[...] = g[:, o : o + n]
-            u_ref[...] = u[:, o : o + n]
+            finish(begin(w.loads(refs[:m], 0, o, n, wg_ref, sem_g)) + begin(w.loads(refs[:m], 1, o, n, wu_ref, sem_u)))
+
+        g, u = dot(a_ref[...], wg_ref[...]), dot(a_ref[...], wu_ref[...])
+        g_ref[...] = g
+        u_ref[...] = u
         act_ref[...] = (g * jax.nn.sigmoid(g) * u).astype(BF16)
 
     return call(
-        kernel, (t // bt,), [rows(bt, d)] + [ANY] * m,
-        [rows(bt, f)] + [rows(bt, n) for _, n in cut] * 2,
-        [sds((t, f), BF16)] + [sds((t, n), F32) for _, n in cut] * 2,
-        4 * t * d * f, 10 * t * f, [pltpu.VMEM((d, f), BF16)] * 2 + [SEM] * 2,
+        kernel, (t // bt,), [rows(bt, d)] + [ANY] * m, [rows(bt, n)] * 3,
+        [sds((t, n), BF16), sds((t, n), F32), sds((t, n), F32)],
+        4 * t * d * n, 10 * t * n, [pltpu.VMEM((d, n), BF16)] * 2 + [SEM] * 2,
     )(a, *w.arrays)
 
 
-def down(act, w, h, bt=512):
-    t, f = act.shape
-    d = h.shape[1]
-
-    def kernel(act_ref, mine, theirs, h_ref, o_ref, a_ref, at_ref, wd_ref, sem):
+def down(acts, w, h, cut, bt=512):
+    t, d = h.shape
+    f, k = cut[-1][0] + cut[-1][1], len(cut)
+
+    def kernel(*refs):
+        mine, theirs, h_ref, o_ref, a_ref, at_ref, wd_ref, sem = refs[k:]
+
         @pl.when(pl.program_id(0) == 0)
         def _():
             finish(w.load_rows((mine, theirs), 0, f, wd_ref, sem))
 
-        o = h_ref[...] + dot(act_ref[...], wd_ref[...]).astype(BF16)
+        total = sum(dot(r[...], wd_ref[o : o + n, :]) for r, (o, n) in zip(refs[:k], cut))
+        o = h_ref[...] + total.astype(BF16)
         o_ref[...] = o
         a = normed(o)
         a_ref[...] = a
         at_ref[...] = a.T
 
     return call(
-        kernel, (t // bt,), [rows(bt, f), ANY, ANY, rows(bt, d)], [rows(bt, d), rows(bt, d), cols(d, bt)],
+        kernel, (t // bt,), [rows(bt, n) for _, n in cut] + [ANY, ANY, rows(bt, d)], [rows(bt, d), rows(bt, d), cols(d, bt)],
         [sds((t, d), BF16), sds((t, d), BF16), sds((d, t), BF16)], 2 * t * d * f, 2 * t * f, [pltpu.VMEM((f, d), BF16), SEM],
-    )(act, *w.arrays, h)
+    )(*acts, *w.arrays, h)
 
 
 def gated_back(g, u, by):
@@ -276,7 +300,7 @@
     k, m = len(cut), len(w.arrays)
 
     def kernel(*refs):
-        h_ref, dy_ref, o_ref, ot_ref, wg_ref, wu_ref, sem_g, sem_u = refs[2 * k + m :]
+        h_ref, dy_ref, o_ref, wg_ref, wu_ref, sem_g, sem_u = refs[2 * k + m :]
 
         @pl.when(pl.program_id(0) == 0)
         def _():
@@ -289,28 +313,35 @@
         wide = h_ref[...].astype(F32)
         scale = lax.rsqrt(jnp.mean(wide * wide, -1, keepdims=True) + 1e-6)
         along = jnp.mean(by * wide, -1, keepdims=True) * (scale * scale * scale)
-        o = dy_ref[...] + (by * scale - wide * along).astype(BF16)
-        o_ref[...] = o
-        ot_ref[...] = o.T
+        o_ref[...] = dy_ref[...] + (by * scale - wide * along).astype(BF16)
 
     return call(
         kernel, (t // bt,), [rows(bt, n) for _, n in cut] * 2 + [ANY] * m + [rows(bt, d)] * 2,
-        [rows(bt, d), cols(d, bt)], [sds((t, d), BF16), sds((d, t), BF16)],
-        4 * t * d * f, 4 * t * f, [pltpu.VMEM((d, f), BF16)] * 2 + [SEM] * 2,
+        rows(bt, d), sds((t, d), BF16), 4 * t * d * f, 4 * t * f, [pltpu.VMEM((d, f), BF16)] * 2 + [SEM] * 2,
     )(*dgs, *dus, *w.arrays, h, dy)
 
 
-def down_grad(byt, act, bn=640):
-    d, t = byt.shape
-    f = act.shape[1]
-
-    def kernel(l_ref, r_ref, o_ref):
-        o_ref[...] = dot(l_ref[...], r_ref[...]).astype(BF16).T
-
-    return call(
-        kernel, (f // bn,), [whole((d, t)), cols(t, bn)], rows(bn, d), sds((f, d), BF16),
-        2 * t * d * f, 2 * t * f + 2 * t * d,
-    )(byt, act)
+def down_grad(by, acts, bn=640):
+    t, d = by.shape
+    counts = [a.shape[1] // bn for a in acts]
+    firsts = [sum(counts[:i]) for i in range(len(acts))]
+    steps = sum(counts)
+
+    def kernel(by_ref, *refs):
+        o_ref = refs[-1]
+        for r, first, count in zip(refs, firsts, counts):
+
+            @pl.when((pl.program_id(0) >= first) & (pl.program_id(0) < first + count))
+            def _():
+                o_ref[...] = dot_tn(r[...], by_ref[...]).astype(BF16)
+
+    def of(first, count):
+        return lambda i: (0, jnp.clip(i - first, 0, count - 1))
+
+    return call(
+        kernel, (steps,), [whole((t, d))] + [pl.BlockSpec((t, bn), of(f, c)) for f, c in zip(firsts, counts)],
+        rows(bn, d), sds((steps * bn, d), BF16), 2 * t * d * steps * bn, 2 * t * steps * bn + 2 * t * d,
+    )(by, *acts)
 
 
 def adamw(w, m, v, g):
@@ -356,7 +387,7 @@
         + [pl.BlockSpec((br, g.shape[1]), of(l)) for l in range(layers) for g in grads[l]],
         [block] * (3 * k),
         [sds(w.shape, BF16) for w in ws] + [sds(w.shape, F32) for w in ws] * 2,
-        20 * k * size, 24 * k * size,
+        20 * k * size, 24 * k * size, mib=MIB,
     )(factor, *ws, *ms, *vs, *(g for l in grads for g in l))
 
 
@@ -366,11 +397,8 @@
 
     def step(x, dy, *arrays):
         weights, m, v = (arrays[i : i + 3] for i in (0, 3, 6))
-        core = lax.axis_index("rep") % 2
-
-        def fetched(shards, columns=slice(None)):
-            halves = [lax.dynamic_slice_in_dim(w[:, columns], core * (w.shape[0] // 2), w.shape[0] // 2, 0) for w in shards]
-            half = halves[0] if len(halves) == 1 else jnp.concatenate(halves)
+
+        def fetched(half):
             mine = lax.all_gather(half, "dp", axis=0, tiled=False)
             return [mine, lax.ppermute(mine, "rep", pairs)]
 
@@ -381,31 +409,47 @@
             return sum(jnp.sum(g.astype(F32) ** 2) for g in gs)
 
         x, dy = x[0], dy[0]
-        cut0, cut1 = pieces(weights[0].shape[2], 2), pieces(weights[0].shape[2], 3)
-        k0 = len(cut0)
-        edge = cut1[1][0]
-        gu0 = Halves(fetched([weights[0][0], weights[1][0]]), [0], 2)
-        d0 = Halves(fetched([weights[2][0]]), [0], 1)
-        d1 = Halves(fetched([weights[2][1]]), [0], 1)
-        first = fetched([weights[0][1], weights[1][1]], slice(0, edge))
-        rest = fetched([weights[0][1], weights[1][1]], slice(edge, None))
-        gu1 = Halves(first + rest, [0, edge], 2)
+        f = weights[0].shape[2]
+        cut0, cut1 = pieces(f, (2, 3)), pieces(f, (8, 10, 7))
+        split, edge = cut0[1][0], cut1[1][0]
+        gate, up_, down_ = weights
+        d = down_.shape[2]
+        up_height, down_height = gate.shape[1] // 2, down_.shape[1] // 2
+        (half,) = halve([[(gate, 0, 0, split), (up_, 0, 0, split)]])
+        gu0a = fetched(half)
+        halves = halve(
+            [
+                [(gate, 0, split, f - split), (up_, 0, split, f - split)],
+                [(down_, 0, 0, d)],
+                [(down_, 1, 0, d), (gate, 1, 0, edge), (up_, 1, 0, edge)],
+                [(gate, 1, edge, f - edge), (up_, 1, edge, f - edge)],
+            ]
+        )
+        gu0b = fetched(halves[0])
+        d0 = Halves(fetched(halves[1]), [0], down_height)
+        first, rest = fetched(halves[2]), fetched(halves[3])
+        d1 = Halves(first, [0], down_height)
+        gu1 = Halves(first + rest, [0, edge], up_height, [down_height, 0])
 
         a0, a0t, dyt = prepare(x, dy)
-        act0, *gu = up(a0, gu0, cut0)
-        h1, a1, a1t = down(act0, d0, x)
+        act0a, g0a, u0a = up(a0, Halves(gu0a, [0], up_height), *cut0[0])
+        act0b, g0b, u0b = up(a0, Halves(gu0b, [split], up_height), *cut0[1])
+        h1, a1, a1t = down([act0a, act0b], d0, x, cut0)
         dgs, dus, up1, so_far = [], [], [], []
         for o, n in cut1:
-            w = Halves(first, [0], 2) if o + n <= edge else Halves(rest, [edge], 2)
+            w = Halves(first, [0], up_height, [down_height]) if o + n <= edge else Halves(rest, [edge], up_height)
             dg, du, g, so_far = last_piece(a1, a1t, dy, dyt, w, d1, o, n, so_far)
             so_far = [so_far]
             dgs.append(dg)
             dus.append(du)
             up1.append(scattered(g))
         down1 = scattered(so_far[0])
-        by, byt = input_back(dgs, dus, gu1, h1, dy, cut1)
-        down0 = scattered(down_grad(byt, act0))
-        up0 = [scattered(first_piece(a0t, gu[j], gu[k0 + j], by, d0, o)) for j, (o, n) in enumerate(cut0)]
+        by = input_back(dgs, dus, gu1, h1, dy, cut1)
+        down0 = scattered(down_grad(by, [act0a, act0b]))
+        up0 = [
+            scattered(first_piece(a0t, g0a, u0a, by, d0, cut0[0][0])),
+            scattered(first_piece(a0t, g0b, u0b, by, d0, cut0[1][0], 256)),
+        ]
 
         total = lax.psum(squares(up1) + squares([down1]) + squares([down0]) + squares(up0), "dp")
         count = lax.psum(1, "dp") * sum(w.size for w in weights)

time: 1020 us -> 997 us (0.977)
  local copies, waits for them, and re-layouts: 14.8 us -> 0 us
    all_gather x5, waiting for transfers between devices: 195 us -> 168 us  [fetched(): mine = lax.all_gather(half, 'dp', axis=0, tiled=False)]
    reduce_scatter x7, waiting for transfers between devices: 132 us -> 149 us  [scattered(): return lax.psum_scatter(g, 'dp', scatter_dimension=0, tiled=True)]
    pallas_call x3 -> x6, Pallas kernels: 150 us -> 158 us  [the longest x2 74.9 us: up(): call(kernel, (t // bt,), [rows(bt, d)] + [ANY] * m, [rows(bt, n)] * 3, [s...]
  transfers between devices with their start and end apart: 17 -> 17, of which waited for: 8 -> 8; matrix products, arithmetic and copies ran while one was open for 2% -> 2% of each run, Pallas kernels for 57% -> 43%
where the time goes in v2:
time: 997 us; the launch traced here: 990 us
  Pallas kernels  620 us (62%)
  waiting for transfers between devices  321 us (32%)
  between operations  20.2 us (2%)
  other arithmetic  18.7 us (2%)
    pallas_call x3, Pallas kernels, last_piece(): call(kernel, (steps,), [rows(bt, d), cols(d, bt)] * 2 + [ANY] * (m + 2 +...  213 us
    all_gather x5, waiting for transfers between devices, fetched(): mine = lax.all_gather(half, 'dp', axis=0, tiled=False)  168 us
    reduce_scatter x7, waiting for transfers between devices, scattered(): return lax.psum_scatter(g, 'dp', scatter_dimension=0, tiled=True)  149 us
    pallas_call x2, Pallas kernels, first_piece(): call(kernel, (steps,), [cols(d, bt), rows(bt, n), rows(bt, n), rows(bt, d...  118 us
    pallas_call x2, Pallas kernels, up(): call(kernel, (t // bt,), [rows(bt, d)] + [ANY] * m, [rows(bt, n)] * 3, [s...  74.9 us
    pallas_call x1, Pallas kernels, input_back(): call(kernel, (t // bt,), [rows(bt, n) for _, n in cut] * 2 + [ANY] * m +...  72.7 us
    pallas_call x2, Pallas kernels, update(): call(kernel, (layers, steps), [pl.BlockSpec(memory_space=pltpu.SMEM)] + [...  41.5 us
    pallas_call x1, Pallas kernels, down(): call(kernel, (t // bt,), [rows(bt, n) for _, n in cut] + [ANY, ANY, rows(...  40.7 us
  transfers between devices with their start and end apart: 17, of which 8 were waited for; matrix products, arithmetic and copies ran while one was open for 2% of the time, Pallas kernels for 43%

profile of v2, /device:TPU:112, one launch (start us, length us, event | category | flops | bytes accessed | tf_op | source)
XLA Modules:
  0.0 990.4 jit_solution(10507410548462071554)
XLA Ops:
  9.5 4.4 shard_map.181
  16.1 28.1 %all-gather.11.cloned.1.call-done = bf16[1024,1280]{1,0:T(8,128)(2,1)} async-done(((bf16[256,1280]{1,0:T(8,128)(2,1)}), bf16[1024,1280]{1,0:T(8,128)(2,1)}) %all-gather.11.cloned.1.call-update) | async-done | bytes 2621456 | tf_op jit(solution)/shard_map/all_gather | solution.py:402
  44.1 44.2 %all-gather.13.cloned.1.call-done = bf16[1024,1920]{1,0:T(8,128)(2,1)} async-done(((bf16[256,1920]{1,0:T(8,128)(2,1)}), bf16[1024,1920]{1,0:T(8,128)(2,1)}) %all-gather.13.cloned.1.call-update) | async-done | bytes 3932176 | tf_op jit(solution)/shard_map/all_gather | solution.py:402
  88.3 17.2 %shard_map.178 = (bf16[4096,1024]{1,0:T(8,128)(2,1)}, bf16[1024,4096]{1,0:T(8,128)(2,1)}, bf16[1024,4096]{1,0:T(8,128)(2,1)}) custom-call(bf16[4096,1024]{1,0:T(8,128)(2,1)} %bitcast.8, bf16[4096,1024]{1,0:T(8,128)(2,1)} %bitcast.10), custom_call_target="tpu_custom_call" | custom-call | flops 33554432 | bytes 41943040 | tf_op jit(solution)/shard_map/pallas_call | solution.py:163
  105.5 21.7 %all-gather.15.cloned.1.call-done = bf16[1600,1024]{1,0:T(8,128)(2,1)} async-done(((bf16[400,1024]{1,0:T(8,128)(2,1)}), bf16[1600,1024]{1,0:T(8,128)(2,1)}) %all-gather.15.cloned.1.call-update) | async-done | bytes 3276816 | tf_op jit(solution)/shard_map/all_gather | solution.py:402
  127.2 30.6 %shard_map.180 = (bf16[4096,1280]{1,0:T(8,128)(2,1)}, f32[4096,1280]{1,0:T(8,128)}, f32[4096,1280]{1,0:T(8,128)}) custom-call(bf16[4096,1024]{1,0:T(8,128)(2,1)} %get-tuple-element.46.a_ref, bf16[4,256,1280]{2,1,0:T(8,128)(2,1)} %bitcast.32, bf16[4,256,1280]{2,1,0:T(8,128)(2,1)} %collective-permute-done.refs_1_), custom_call_target="tpu_custom_call" | custom-call | flops 21474836480 | bytes 52428800 | tf_op jit(solution)/shard_map/pallas_call | solution.py:185
  157.8 17.9 %all-gather.19.cloned.1.call-done = bf16[1024,2176]{1,0:T(8,128)(2,1)} async-done(((bf16[256,2176]{1,0:T(8,128)(2,1)}), bf16[1024,2176]{1,0:T(8,128)(2,1)}) %all-gather.19.cloned.1.call-update) | async-done | bytes 4456464 | tf_op jit(solution)/shard_map/all_gather | solution.py:402
  175.7 56.3 %all-gather.17.cloned.1.call-done = bf16[2624,1024]{1,0:T(8,128)(2,1)} async-done(((bf16[656,1024]{1,0:T(8,128)(2,1)}), bf16[2624,1024]{1,0:T(8,128)(2,1)}) %all-gather.17.cloned.1.call-update) | async-done | bytes 5373968 | tf_op jit(solution)/shard_map/all_gather | solution.py:402
  232.0 44.3 %shard_map.182 = (bf16[4096,1920]{1,0:T(8,128)(2,1)}, f32[4096,1920]{1,0:T(8,128)}, f32[4096,1920]{1,0:T(8,128)}) custom-call(bf16[4096,1024]{1,0:T(8,128)(2,1)} %get-tuple-element.46.a_ref, bf16[4,256,1920]{2,1,0:T(8,128)(2,1)} %bitcast.26, bf16[4,256,1920]{2,1,0:T(8,128)(2,1)} %collective-permute-done.1.refs_1_), custom_call_target="tpu_custom_call" | custom-call | flops 32212254720 | bytes 78643200 | tf_op jit(solution)/shard_map/pallas_call | solution.py:185
  276.3 40.7 %shard_map.183 = (bf16[4096,1024]{1,0:T(8,128)(2,1)}, bf16[4096,1024]{1,0:T(8,128)(2,1)}, bf16[1024,4096]{1,0:T(8,128)(2,1)}) custom-call(bf16[4096,1280]{1,0:T(8,128)(2,1)} %get-tuple-element.47.refs_0_, bf16[4096,1920]{1,0:T(8,128)(2,1)} %get-tuple-element.49.refs_1_, bf16[4,400,1024]{2,1,0:T(8,128)(2,1)} %bitcast.28, ...), custom_call_target="tpu_custom_call" | custom-call | flops 26843545600 | bytes 26214400 | tf_op jit(solution)/shard_map/pallas_call | solution.py:210
  317.1 66.6 %shard_map.184 = (bf16[4096,1024]{1,0:T(8,128)(2,1)}, bf16[4096,1024]{1,0:T(8,128)(2,1)}, bf16[1024,2048]{1,0:T(8,128)(2,1)}, bf16[3200,1024]{1,0:T(8,128)(2,1)}) custom-call(bf16[4096,1024]{1,0:T(8,128)(2,1)} %get-tuple-element.51.a_ref, bf16[1024,4096]{1,0:T(8,128)(2,1)} %get-tuple-element.52.at_ref, bf16[4096,1024]{1,0:T(8,128)(2,1)} %bitcast.11, ...), custom_call_target="tpu_custom_call" | custom-call | flops 51539607552 | bytes 50331648 | tf_op jit(solution)/shard_map/pallas_call | solution.py:255
  383.7 81.2 %shard_map.185 = (bf16[4096,1280]{1,0:T(8,128)(2,1)}, bf16[4096,1280]{1,0:T(8,128)(2,1)}, bf16[1024,2560]{1,0:T(8,128)(2,1)}, bf16[3200,1024]{1,0:T(8,128)(2,1)}) custom-call(bf16[4096,1024]{1,0:T(8,128)(2,1)} %get-tuple-element.51.a_ref, bf16[1024,4096]{1,0:T(8,128)(2,1)} %get-tuple-element.52.at_ref, ...), custom_call_target="tpu_custom_call", output_to_operand_aliasing={{3}: (8, {})} | custom-call | flops 64424509440 | bytes 54525952 | tf_op jit(solution)/shard_map/pallas_call | solution.py:255
  464.9 65.6 %shard_map.186 = (bf16[4096,896]{1,0:T(8,128)(2,1)}, bf16[4096,896]{1,0:T(8,128)(2,1)}, bf16[1024,1792]{1,0:T(8,128)(2,1)}, bf16[3200,1024]{1,0:T(8,128)(2,1)}) custom-call(bf16[4096,1024]{1,0:T(8,128)(2,1)} %get-tuple-element.51.a_ref, bf16[1024,4096]{1,0:T(8,128)(2,1)} %get-tuple-element.52.at_ref, ...), custom_call_target="tpu_custom_call", output_to_operand_aliasing={{3}: (8, {})} | custom-call | flops 45097156608 | bytes 48234496 | tf_op jit(solution)/shard_map/pallas_call | solution.py:255
  532.3 72.7 %shard_map.187.by_ref = bf16[4096,1024]{1,0:T(8,128)(2,1)} custom-call(bf16[4096,1024]{1,0:T(8,128)(2,1)} %get-tuple-element.62.refs_0_, bf16[4096,1280]{1,0:T(8,128)(2,1)} %get-tuple-element.63.refs_1_, bf16[4096,896]{1,0:T(8,128)(2,1)} %get-tuple-element.64.refs_2_, bf16[4096,1024]{1,0:T(8,128)(2,1)} %get-tuple-element.65.refs_3_, ...), custom_call_target="tpu_custom_call" | custom-call | flops 53687091200 | bytes 52428800 | tf_op jit(solution)/shard_map/pallas_call | solution.py:318
  605.0 46.2 %shard_map.189 = bf16[1024,2560]{1,0:T(8,128)(2,1)} custom-call(bf16[1024,4096]{1,0:T(8,128)(2,1)} %get-tuple-element.69.at_ref, f32[4096,1280]{1,0:T(8,128)} %get-tuple-element.70.g_ref, f32[4096,1280]{1,0:T(8,128)} %get-tuple-element.71.u_ref, bf16[4096,1024]{1,0:T(8,128)(2,1)} %shard_map.187.by_ref, bf16[4,400,1024]{2,1,0:T(8,128)(2,1)} %bitcast.29, ...), custom_call_target="tpu_custom_call" | custom-call | flops 32212254720 | bytes 58720256 | tf_op jit(solution)/shard_map/pallas_call | solution.py:290
  652.0 35.9 %shard_map.188 = bf16[3200,1024]{1,0:T(8,128)(2,1)} custom-call(bf16[4096,1024]{1,0:T(8,128)(2,1)} %shard_map.187.by_ref, bf16[4096,1280]{1,0:T(8,128)(2,1)} %get-tuple-element.47.refs_0_, bf16[4096,1920]{1,0:T(8,128)(2,1)} %get-tuple-element.49.refs_1_), custom_call_target="tpu_custom_call" | custom-call | flops 26843545600 | bytes 34603008 | tf_op jit(solution)/shard_map/pallas_call | solution.py:341
  688.0 71.3 %shard_map.190 = bf16[1024,3840]{1,0:T(8,128)(2,1)} custom-call(bf16[1024,4096]{1,0:T(8,128)(2,1)} %get-tuple-element.69.at_ref, f32[4096,1920]{1,0:T(8,128)} %get-tuple-element.72.g_ref, f32[4096,1920]{1,0:T(8,128)} %get-tuple-element.73.u_ref, bf16[4096,1024]{1,0:T(8,128)(2,1)} %shard_map.187.by_ref, bf16[4,400,1024]{2,1,0:T(8,128)(2,1)} %bitcast.30, ...), custom_call_target="tpu_custom_call" | custom-call | flops 48318382080 | bytes 79691776 | tf_op jit(solution)/shard_map/pallas_call | solution.py:290
  771.3 16.4 %reduce-scatter.14.cloned.1.call-done.refs_5_ = bf16[800,1024]{1,0:T(8,128)(2,1)} async-done(((bf16[3200,1024]{1,0:T(8,128)(2,1)}), bf16[800,1024]{1,0:T(8,128)(2,1)}) %reduce-scatter.14.cloned.1.call-update) | async-done | bytes 1638416 | tf_op jit(solution)/shard_map/reduce_scatter | solution.py:406
  791.2 61.1 %reduce-scatter.16.cloned.1.call-done.refs_4_ = bf16[800,1024]{1,0:T(8,128)(2,1)} async-done(((bf16[3200,1024]{1,0:T(8,128)(2,1)}), bf16[800,1024]{1,0:T(8,128)(2,1)}) %reduce-scatter.16.cloned.1.call-update) | async-done | bytes 1638416 | tf_op jit(solution)/shard_map/reduce_scatter | solution.py:406
  855.8 71.1 %reduce-scatter.20.cloned.1.call-done.refs_8_ = bf16[256,3840]{1,0:T(8,128)(2,1)} async-done(((bf16[1024,3840]{1,0:T(8,128)(2,1)}), bf16[256,3840]{1,0:T(8,128)(2,1)}) %reduce-scatter.20.cloned.1.call-update) | async-done | bytes 1966096 | tf_op jit(solution)/shard_map/reduce_scatter | solution.py:406
  926.9 3.2 multiply_reduce_fusion
  931.4 9.4 psum.7
  941.5 16.1 %shard_map.192 = (bf16[2,800,1024]{2,1,0:T(8,128)(2,1)}, f32[2,800,1024]{2,1,0:T(8,128)}, f32[2,800,1024]{2,1,0:T(8,128)}) custom-call(f32[1,1]{1,0:T(1,128)} %bitcast.7.refs_0_, bf16[2,800,1024]{2,1,0:T(8,128)(2,1)} %refs_1_.7, f32[2,800,1024]{2,1,0:T(8,128)} %refs_2_.5, f32[2,800,1024]{2,1,0:T(8,128)} %refs_3_.5, ...), custom_call_target="tpu_custom_call" | custom-call | flops 32768000 | bytes 39321600 | tf_op jit(solution)/shard_map/pallas_call | solution.py:384
  957.7 25.4 %shard_map.191 = (bf16[2,256,3200]{2,1,0:T(8,128)(2,1)}, bf16[2,256,3200]{2,1,0:T(8,128)(2,1)}, f32[2,256,3200]{2,1,0:T(8,128)}, f32[2,256,3200]{2,1,0:T(8,128)}...) custom-call(f32[1,1]{1,0:T(1,128)} %bitcast.7.refs_0_, bf16[2,256,3200]{2,1,0:T(8,128)(2,1)} %refs_1_.6, ...), custom_call_target="tpu_custom_call" | custom-call | flops 65536000 | bytes 78643200 | tf_op jit(solution)/shard_map/pallas_call | solution.py:384
  (45 shorter events, 22.7 us)
Async XLA Ops:
  7.2 36.9 %all-gather.11.cloned.1.call-start = ((), (), s32[]{:S(2)}) async-start(), calls=%async_computation.14 | async-start | bytes 3276800 | tf_op jit(solution)/shard_map/all_gather | solution.py:402
  9.4 78.9 %all-gather.13.cloned.1.call-start = ((), (), s32[]{:S(2)}) async-start(), calls=%async_computation.15 | async-start | bytes 4915200 | tf_op jit(solution)/shard_map/all_gather | solution.py:402
  13.9 113.3 %all-gather.15.cloned.1.call-start = ((), (), s32[]{:S(2)}) async-start(), calls=%async_computation.16 | async-start | bytes 4096000 | tf_op jit(solution)/shard_map/all_gather | solution.py:402
  14.7 161.0 %all-gather.19.cloned.1.call-start = ((), (), s32[]{:S(2)}) async-start(), calls=%async_computation.18 | async-start | bytes 5570560 | tf_op jit(solution)/shard_map/all_gather | solution.py:402
  15.3 216.7 %all-gather.17.cloned.1.call-start = ((), (), s32[]{:S(2)}) async-start(), calls=%async_computation.17 | async-start | bytes 6717440 | tf_op jit(solution)/shard_map/all_gather | solution.py:402
  16.0 743.5 %reduce-scatter.12.cloned.1.call-start = ((), (), s32[]{:S(2)}) async-start(), calls=%async_computation.9 | async-start | bytes 4587520 | tf_op jit(solution)/shard_map/reduce_scatter | solution.py:406
  44.1 83.1 %collective-permute-start = (bf16[4,256,1280]{2,1,0:T(8,128)(2,1)}, bf16[4,256,1280]{2,1,0:T(8,128)(2,1)}, u32[]{:S(2)}, u32[]{:S(2)}) collective-permute-start(bf16[4,256,1280]{2,1,0:T(8,128)(2,1)} %bitcast.31), channel_id=1, source_target_pairs={{0,4},{4,0},{8,12},{12,8},{1,5},{5,1},{9,13},{13,9},{2,6},{6,2},{1... | collective-permute-start | bytes 7864328 | tf_op jit(solution)/shard_map/ppermute | solution.py:403
  88.3 143.7 %collective-permute-start.1 = (bf16[4,256,1920]{2,1,0:T(8,128)(2,1)}, bf16[4,256,1920]{2,1,0:T(8,128)(2,1)}, u32[]{:S(2)}, u32[]{:S(2)}) collective-permute-start(bf16[4,256,1920]{2,1,0:T(8,128)(2,1)} %bitcast.25), channel_id=1, source_target_pairs={{0,4},{4,0},{8,12},{12,8},{1,5},{5,1},{9,13},{13,9},{2,6},{6,2},{1... | collective-permute-start | bytes 11796488 | tf_op jit(solution)/shard_map/ppermute | solution.py:403
  127.2 149.1 %collective-permute-start.2 = (bf16[4,400,1024]{2,1,0:T(8,128)(2,1)}, bf16[4,400,1024]{2,1,0:T(8,128)(2,1)}, u32[]{:S(2)}, u32[]{:S(2)}) collective-permute-start(bf16[4,400,1024]{2,1,0:T(8,128)(2,1)} %bitcast.27), channel_id=1, source_target_pairs={{0,4},{4,0},{8,12},{12,8},{1,5},{5,1},{9,13},{13,9},{2,6},{6,2},{1... | collective-permute-start | bytes 9830408 | tf_op jit(solution)/shard_map/ppermute | solution.py:403
  175.7 208.0 %collective-permute-start.4 = (bf16[4,256,2176]{2,1,0:T(8,128)(2,1)}, bf16[4,256,2176]{2,1,0:T(8,128)(2,1)}, u32[]{:S(2)}, u32[]{:S(2)}) collective-permute-start(bf16[4,256,2176]{2,1,0:T(8,128)(2,1)} %bitcast.21), channel_id=1, source_target_pairs={{0,4},{4,0},{8,12},{12,8},{1,5},{5,1},{9,13},{13,9},{2,6},{6,2},{1... | collective-permute-start | bytes 13369352 | tf_op jit(solution)/shard_map/ppermute | solution.py:403
  232.0 85.1 %collective-permute-start.3 = (bf16[4,656,1024]{2,1,0:T(8,128)(2,1)}, bf16[4,656,1024]{2,1,0:T(8,128)(2,1)}, u32[]{:S(2)}, u32[]{:S(2)}) collective-permute-start(bf16[4,656,1024]{2,1,0:T(8,128)(2,1)} %bitcast.15), channel_id=1, source_target_pairs={{0,4},{4,0},{8,12},{12,8},{1,5},{5,1},{9,13},{13,9},{2,6},{6,2},{1... | collective-permute-start | bytes 16121864 | tf_op jit(solution)/shard_map/ppermute | solution.py:403
  530.6 231.1 %reduce-scatter.8.cloned.1.call-start = ((), (), s32[]{:S(2)}) async-start(), calls=%async_computation.7 | async-start | bytes 5242880 | tf_op jit(solution)/shard_map/reduce_scatter | solution.py:406
  531.4 232.7 %reduce-scatter.10.cloned.1.call-start = ((), (), s32[]{:S(2)}) async-start(), calls=%async_computation.8 | async-start | bytes 6553600 | tf_op jit(solution)/shard_map/reduce_scatter | solution.py:406
  532.2 236.4 %reduce-scatter.18.cloned.1.call-start = ((), (), s32[]{:S(2)}) async-start(), calls=%async_computation.12 | async-start | bytes 6553600 | tf_op jit(solution)/shard_map/reduce_scatter | solution.py:406
  651.3 136.4 %reduce-scatter.14.cloned.1.call-start = ((), (), s32[]{:S(2)}) async-start(), calls=%async_computation.10 | async-start | bytes 8192000 | tf_op jit(solution)/shard_map/reduce_scatter | solution.py:406
  651.9 200.4 %reduce-scatter.16.cloned.1.call-start = ((), (), s32[]{:S(2)}) async-start(), calls=%async_computation.11 | async-start | bytes 8192000 | tf_op jit(solution)/shard_map/reduce_scatter | solution.py:406
  688.0 239.0 %reduce-scatter.20.cloned.1.call-start = ((), (), s32[]{:S(2)}) async-start(), calls=%async_computation.13 | async-start | bytes 9830400 | tf_op jit(solution)/shard_map/reduce_scatter | solution.py:406
Sparse Core Ops, SparseCore 0:
  10.1 33.9 all-gather.10
  46.2 42.0 all-gather.12
  90.4 36.7 all-gather.14
  129.2 46.4 all-gather.18
  177.7 54.2 all-gather.16
  530.7 39.1 reduce-scatter.11
  572.7 42.4 reduce-scatter.7
  618.1 51.0 reduce-scatter.9
  672.1 51.0 reduce-scatter.17
  725.9 61.7 reduce-scatter.13
  790.5 61.7 reduce-scatter.15
  854.5 72.4 reduce-scatter.19
